TPU v7x, 512 devices: a 8x2x16 block of a 8x16x16 slice. The times are simulated.
512 devices in a mesh: chan: 2 (over y), row: 128 (over z, x), col: 2 (over core).
Axes of the slice: x: 8, y: 2, z: 16, core: 2. Of those that a mesh axis runs over, the one named last changes fastest.
The devices are a block of a 8x16x16 slice.
Arguments:
- hamiltonian_rows: float32 [256, 2, 2, 65536], P('chan', 'col', None, 'row'), parts along dimension 0, may hold values from -2 to 2, as said below
- current_block: float32 [131072, 256], P(('chan', 'row', 'col')), parts along dimension 0, may hold values from -6 to 6
- correction_block: float32 [131072, 256], P(('chan', 'row', 'col')), parts along dimension 0, may hold values from -6 to 6
- previous_block: float32 [131072, 256], P(('chan', 'row', 'col')), parts along dimension 0, may hold values from -6 to 6
- ritz_values: float32 [512], P('chan'), parts along dimension 0, may hold values from -2 to 2
- mixing_coeffs: float32 [1536, 256], P('chan'), parts along dimension 0, may hold values from -0.21875 to 0.21875
Outputs:
- next_block: float32 [1024, 256], P(('chan', 'row', 'col')), parts along dimension 0
- next_direction: float32 [1024, 256], P(('chan', 'row', 'col')), parts along dimension 0
- next_correction: float32 [1024, 256], P(('chan', 'row', 'col')), parts along dimension 0
- ritz_matrix: float32 [512, 256], P('chan'), parts along dimension 0
- metric_matrix: float32 [512, 256], P('chan'), parts along dimension 0
There are 2 independent parts, one for each index of `chan`. A program takes and returns all parts, laid end to end along the dimension named above; each array names one. Nothing has to cross between parts.
Inputs may be any that keep to these rules, and one draw needn't show every extreme that they name: hamiltonian_rows[a, b, j, :] is row (a * 2 + b) * 256 + j of the channel's Hamiltonian; its entry in that row's own column is the onsite energy.
All inputs are finite; a program needn't handle non-finite values.
Results may differ from a plain program's by a relative error of at most 0.00008.
Values sent between devices are 32-bit elements; how exact they have to be, the bound alone decides.
No kernel may reach another device: no remote copies, remote signals or barrier semaphores. Data moves between devices by JAX's collectives and lax.ppermute only.
A program may use at most 64 MiB of HBM per device.

v0:
```python
import jax
import jax.numpy as jnp
from jax import lax
from jax.sharding import Mesh
from jax.sharding import PartitionSpec as P

ROW = ("row_0", "row_1")
ROW_COL = ("row_0", "row_1", "col")
CHAN_ROW_COL = ("chan", "row_0", "row_1", "col")


def copy_for_each(shard, axis):
    count = lax.axis_size(axis)
    return lax.all_to_all(
        jnp.broadcast_to(shard[None], (count, *shard.shape)), axis, 0, 0, tiled=True
    )


def laid_out(blocks, dim):
    lengths = list(blocks.shape[1:])
    lengths[dim] *= blocks.shape[0]
    return jnp.moveaxis(blocks, 0, dim).reshape(lengths)


def gather_directly(shard, axis, dim):
    blocks = copy_for_each(shard, axis)
    return laid_out(blocks, dim)


def sum_by_axis(running, axes):
    for axis in axes:
        running = lax.psum_scatter(running, axis, scatter_dimension=0, tiled=True)
    return running


def packed_total(arrays, axis):
    ends = [0]
    for a in arrays:
        ends.append(ends[-1] + a.size)
    running = lax.psum(jnp.concatenate([a.ravel() for a in arrays]), axis)
    return tuple((running[b:e].reshape(a.shape) for a, b, e in zip(arrays, ends, ends[1:])))


def matmul(left, right):
    return jnp.dot(left, right, preferred_element_type=jnp.float32, precision=lax.Precision.HIGHEST)


def tmatmul(left, right):
    return lax.dot_general(
        left,
        right,
        (((0,), (0,)), ((), ())),
        preferred_element_type=jnp.float32,
        precision=lax.Precision.HIGHEST,
    )


def upper_blocks(gram_matrix, block_width):
    pieces = []
    for left_index in range(3):
        for right_index in range(left_index, 3):
            pieces.append(
                gram_matrix[
                    left_index * block_width : (left_index + 1) * block_width,
                    right_index * block_width : (right_index + 1) * block_width,
                ]
            )
    return jnp.stack(pieces)


def full_gram(stacked):
    lookup = {(0, 0): 0, (0, 1): 1, (0, 2): 2, (1, 1): 3, (1, 2): 4, (2, 2): 5}
    row_parts = []
    for left_index in range(3):
        column_parts = []
        for right_index in range(3):
            if left_index <= right_index:
                column_parts.append(stacked[lookup[left_index, right_index]])
            else:
                column_parts.append(stacked[lookup[right_index, left_index]].T)
        row_parts.append(jnp.concatenate(column_parts, axis=1))
    return jnp.concatenate(row_parts, axis=0)


def on_device(
    hamiltonian_rows, current_block, correction_block, previous_block, ritz_values, mixing_coeffs
):
    block_width = current_block.shape[1]
    out_rows = hamiltonian_rows.shape[2]
    window_total = out_rows * lax.axis_size(ROW) * lax.axis_size("col")
    own_rows = jnp.concatenate([current_block, correction_block, previous_block], axis=1)
    window_rows = own_rows[:out_rows]
    basis_part = upper_blocks(tmatmul(window_rows, window_rows), block_width)
    gathered = gather_directly(own_rows, "col", 0)
    local_tile = hamiltonian_rows.reshape(-1, hamiltonian_rows.shape[3])
    product_rows = sum_by_axis(matmul(local_tile, gathered), ROW)
    residual = product_rows[:, :block_width] - window_rows[:, :block_width] * ritz_values[None, :]
    squares = jnp.sum(residual * residual, axis=0)
    product_part = tmatmul(window_rows, product_rows)
    basis_sum, product_sum, square_sum = packed_total((basis_part, product_part, squares), ROW_COL)
    next_block = matmul(window_rows, mixing_coeffs)
    metric_gram = full_gram(basis_sum)
    ritz_matrix = tmatmul(mixing_coeffs, matmul(product_sum, mixing_coeffs))
    metric_matrix = tmatmul(mixing_coeffs, matmul(metric_gram, mixing_coeffs))
    next_direction = matmul(window_rows[:, block_width:], mixing_coeffs[block_width:, :])
    next_correction = residual * lax.rsqrt(square_sum / window_total + 1e-06)
    return (next_block, next_direction, next_correction, ritz_matrix, metric_matrix)


def solution(mesh):
    finer = Mesh(
        mesh.devices.reshape(mesh.shape["chan"], 16, 8, mesh.shape["col"]),
        ("chan", "row_0", "row_1", "col"),
    )
    in_specs = (
        P("chan", "col", None, ROW),
        P(CHAN_ROW_COL, None),
        P(CHAN_ROW_COL, None),
        P(CHAN_ROW_COL, None),
        P("chan"),
        P("chan", None),
    )
    out_specs = (
        P(CHAN_ROW_COL, None),
        P(CHAN_ROW_COL, None),
        P(CHAN_ROW_COL, None),
        P("chan", None),
        P("chan", None),
    )
    return jax.shard_map(
        on_device, mesh=finer, in_specs=in_specs, out_specs=out_specs, check_vma=False
    )
```

profile of v0, /device:TPU:65, one launch (start us, length us, event | category | flops | bytes accessed | tf_op | source)
XLA Modules:
  0.0 563.5 jit_solution(1602862439774385199)
XLA Ops:
  7.2 1.0 constant_dynamic-update-slice_fusion.2
  8.2 1.0 constant_dynamic-update-slice_fusion.1
  9.1 1.0 constant_dynamic-update-slice_fusion
  10.1 0.9 copy-done.1
  11.0 1.3 broadcast_in_dim.2
  12.3 45.1 %all-to-all-start = ((f32[2,256,768]{2,1,0:T(8,128)}), f32[2,256,768]{2,1,0:T(8,128)S(1)}, u32[]{:S(2)}, u32[]{:S(2)}) async-start(f32[2,256,768]{2,1,0:T(8,128)} %broadcast_in_dim.2), calls=%async_computation | async-start | bytes 3145728 | tf_op jit(solution)/shard_map/all_to_all | solution.py:14
  57.4 0.4 reshape.96
  57.7 1.8 all-to-all-done
  59.5 2.6 convolution_bitcast_fusion
  62.1 1.2 copy.51
  63.4 2.9 fusion.26
  66.5 2.0 copy.56
  68.5 1.3 dynamic-slice
  70.4 49.3 %reduce-scatter.5.cloned.1.call-done = f32[16,768]{1,0:T(8,128)} async-done(((f32[256,768]{1,0:T(8,128)}), f32[16,768]{1,0:T(8,128)}) %reduce-scatter.5.cloned.1.call-update) | async-done | bytes 49168
  119.7 1.0 copy.52
  120.7 27.3 %all-reduce = f32[16,768]{0,1:T(8,128)S(1)} all-reduce(f32[16,768]{0,1:T(8,128)S(1)} %copy.52), channel_id=3, replica_groups=mesh['chan'=2,'row_0'=16,'row_1'=8,'col'=2] {'row_1'}, use_global_device_ids=true, to_apply=%region_1.0.clone | all-reduce | flops 12288 | bytes 98304
  147.9 0.1 constant_dynamic-slice_fusion
  148.0 2.9 fusion.16
  151.0 0.1 copy.55
  151.1 1.6 reshape.98
  152.6 0.7 multiply_reduce_fusion
  153.3 4.3 pad_maximum_fusion
  157.7 1.1 copy-done
  158.8 0.1 copy-done.3
  158.9 0.9 fusion.14
  159.8 1.7 fusion.28
  161.5 371.7 %all-reduce.3.cloned.1.call-done = f32[983296]{0:T(1024)} async-done(((f32[983296]{0:T(1024)}), f32[983296]{0:T(1024)}) %all-reduce.3.cloned.1.call-update) | async-done | bytes 3933200 | tf_op jit(solution)/shard_map/psum | solution.py:40
  533.2 0.7 fusion.31
  533.9 1.3 broadcast_multiply_fusion
  535.2 3.3 slice.176
  538.4 2.7 reshape.99
  541.1 2.0 fusion.36
  543.1 1.5 convolution_bitcast_fusion.2
  544.6 0.8 copy.49
  545.4 1.4 fusion.35
  546.9 0.1 slice.157
  546.9 0.1 slice.165
  547.0 0.1 slice.161
  547.1 0.1 slice.159
  547.2 0.1 copy.46
  547.3 0.1 slice.167
  547.4 0.8 copy.47
  548.2 0.1 slice.163
  548.3 0.8 copy.45
  549.2 0.3 copy.48
  549.5 4.9 fusion
  554.4 1.5 convolution_bitcast_fusion.1
  555.8 0.8 copy.50
  (20 shorter events, 0.4 us)
Async XLA Ops:
  10.1 0.9 copy-start.1
  11.0 46.4 %copy-start.4 = (f32[128,1,2,512]{3,2,1,0:T(2,128)S(1)}, f32[128,1,2,512]{3,2,1,0:T(2,128)}, u32[]{:S(2)}) copy-start(f32[128,1,2,512]{3,2,1,0:T(2,128)} %param.6) | copy-start | bytes 1572868
  12.3 47.2 %all-to-all-start = ((f32[2,256,768]{2,1,0:T(8,128)}), f32[2,256,768]{2,1,0:T(8,128)S(1)}, u32[]{:S(2)}, u32[]{:S(2)}) async-start(f32[2,256,768]{2,1,0:T(8,128)} %broadcast_in_dim.2), calls=%async_computation | async-start | bytes 3145728 | tf_op jit(solution)/shard_map/all_to_all | solution.py:14
  57.4 62.3 %reduce-scatter.5.cloned.1.call-start = ((), (), s32[]{:S(2)}) async-start(), calls=%async_computation.3 | async-start | bytes 835584
  63.3 469.9 %all-reduce.3.cloned.1.call-start = ((), (), s32[]{:S(2)}) async-start(), calls=%async_computation.2 | async-start | bytes 7872512 | tf_op jit(solution)/shard_map/psum | solution.py:40
  151.1 1.6 copy-start.5
  157.6 1.1 copy-start
  157.6 1.2 copy-start.2
  157.6 1.3 copy-start.3
Sparse Core Ops, SparseCore 0:
  63.5 56.1 reduce-scatter.4
  157.8 375.3 all-reduce.2
where the time goes:
time: 564 us
  waiting for transfers between devices  423 us (75%)
  starting transfers between devices  45.2 us (8%)
  blocking collectives  27.3 us (5%)
  local copies, waits for them, and re-layouts  25.4 us (5%)
  matrix products  20.9 us (4%)
  between operations  14.9 us (3%)
  other arithmetic  7.02 us (1%)
    psum x1, waiting for transfers between devices, packed_total(): running = lax.psum(jnp.concatenate([a.ravel() for a in arrays]), axis)  372 us
    unnamed x3, waiting for transfers between devices  49.4 us
    all_to_all x1, starting transfers between devices, copy_for_each(): lax.all_to_all(jnp.broadcast_to(shard[None], (count, *shard.shape)), axis...  45.1 us
    unnamed x1, blocking collectives  27.3 us
    dot_general x5, matrix products, matmul(): jnp.dot(left, right, preferred_element_type=jnp.float32, precision=lax.Pr...  12.1 us
  transfers between devices with their start and end apart: 3, of which 3 were waited for; matrix products, arithmetic and copies ran while one was open for 2% of the time, Pallas kernels for 0%

commit v1 on v0

v1 whole, which is shorter than its diff:
```python
import jax
import jax.numpy as jnp
from jax import lax
from jax.sharding import Mesh
from jax.sharding import PartitionSpec as P

ROW = ("row_0", "row_1")
CHAN_ROW_COL = ("chan", "row_0", "row_1", "col")
LANES = 128


def exchange(blocks, axis):
    return lax.all_to_all(blocks, axis, 0, 0, tiled=True)


def copies(shard, axis):
    return exchange(jnp.broadcast_to(shard[None], (lax.axis_size(axis), *shard.shape)), axis)


def swap_cores(shard):
    return lax.ppermute(shard, "col", [(0, 1), (1, 0)])


def matmul(left, right):
    return jnp.dot(left, right, preferred_element_type=jnp.float32, precision=lax.Precision.HIGHEST)


def tmatmul(left, right):
    return lax.dot_general(
        left,
        right,
        (((0,), (0,)), ((), ())),
        preferred_element_type=jnp.float32,
        precision=lax.Precision.HIGHEST,
    )


def on_device(
    hamiltonian_rows, current_block, correction_block, previous_block, ritz_values, mixing_coeffs
):
    n_z, n_x, n_c = (lax.axis_size(a) for a in ("row_0", "row_1", "col"))
    width = current_block.shape[1]
    own_len = current_block.shape[0]
    out_rows = hamiltonian_rows.shape[2]
    window_total = out_rows * n_z * n_x * n_c
    core = lax.axis_index("col")

    direction = matmul(correction_block, mixing_coeffs[width : 2 * width]) + matmul(
        previous_block, mixing_coeffs[2 * width :]
    )
    mixed = matmul(current_block, mixing_coeffs[:width]) + direction
    next_block = mixed[:out_rows]
    next_direction = direction[:out_rows]

    own = jnp.concatenate([current_block, mixed], axis=1)
    other = swap_cores(own)
    tile = hamiltonian_rows.reshape(n_z, n_x, out_rows, n_c * own_len)
    tile = tile.transpose(1, 0, 2, 3).reshape(n_x * n_z * out_rows, n_c * own_len)
    own_tile = lax.dynamic_slice_in_dim(tile, core * own_len, own_len, 1)
    other_tile = lax.dynamic_slice_in_dim(tile, (1 - core) * own_len, own_len, 1)
    partial = matmul(own_tile, own) + matmul(other_tile, other)

    by_x = exchange(partial.reshape(n_x, n_z * out_rows, 2 * width), "row_1").sum(axis=0)
    lines = out_rows * 2 * width // LANES
    summed = exchange(by_x.reshape(n_z, lines, LANES), "row_0").sum(axis=0)
    summed = summed.reshape(out_rows, 2 * width)
    residual = summed[:, :width] - current_block[:out_rows] * ritz_values[None, :]
    squares = jnp.sum(residual * residual, axis=0)

    mine = jnp.concatenate(
        [
            summed[:, width:].reshape(-1, LANES),
            next_block.reshape(-1, LANES),
            squares.reshape(-1, LANES),
        ],
        axis=0,
    )
    n_lines = out_rows * width // LANES
    by_z = copies(mine, "row_0")
    square_z = by_z[:, 2 * n_lines :].sum(axis=0)
    rows_z = by_z[:, : 2 * n_lines].reshape(-1, LANES)
    gathered = copies(jnp.concatenate([rows_z, square_z], axis=0), "row_1")
    partner = swap_cores(gathered)

    def split(block):
        rows = block[:, : n_z * 2 * n_lines].reshape(n_x, n_z, 2, n_lines, LANES)
        product = rows[:, :, 0].reshape(-1, width)
        window = rows[:, :, 1].reshape(-1, width)
        grams = tmatmul(window, jnp.concatenate([product, window], axis=1))
        return grams, block[:, n_z * 2 * n_lines :].sum(axis=0)

    own_grams, own_squares = split(gathered)
    partner_grams, partner_squares = split(partner)
    grams = own_grams + partner_grams
    square_sum = (own_squares + partner_squares).reshape(width)
    next_correction = residual * lax.rsqrt(square_sum / window_total + 1e-06)
    return (next_block, next_direction, next_correction, grams[:, :width], grams[:, width:])


def solution(mesh):
    finer = Mesh(
        mesh.devices.reshape(mesh.shape["chan"], 16, 8, mesh.shape["col"]),
        ("chan", "row_0", "row_1", "col"),
    )
    in_specs = (
        P("chan", "col", None, ROW),
        P(CHAN_ROW_COL, None),
        P(CHAN_ROW_COL, None),
        P(CHAN_ROW_COL, None),
        P("chan"),
        P("chan", None),
    )
    out_specs = (
        P(CHAN_ROW_COL, None),
        P(CHAN_ROW_COL, None),
        P(CHAN_ROW_COL, None),
        P("chan", None),
        P("chan", None),
    )
    return jax.shard_map(
        on_device, mesh=finer, in_specs=in_specs, out_specs=out_specs, check_vma=False
    )
```

time: 564 us -> 135 us (0.24)
  waiting for transfers between devices: 423 us -> 24.6 us
  local copies, waits for them, and re-layouts: 25.4 us -> 5.97 us
  starting transfers between devices: 45.2 us -> 61.6 us
  matrix products: 20.9 us -> 5.58 us
  between operations: 14.9 us -> 0.94 us
  blocking collectives: 27.3 us -> 35.2 us
  other arithmetic: 7.02 us -> 0.81 us
    psum x1 -> x0, waiting for transfers between devices: 372 us -> none  [packed_total(): running = lax.psum(jnp.concatenate([a.ravel() for a in arrays]), axis)]
    ppermute x0 -> x2, starting transfers between devices: none -> 51.4 us  [swap_cores(): return lax.ppermute(shard, 'col', [(0, 1), (1, 0)])]
    unnamed x3 -> x0, waiting for transfers between devices: 49.4 us -> none
    all_to_all x0 -> x2, blocking collectives: none -> 35.2 us  [exchange(): return lax.all_to_all(blocks, axis, 0, 0, tiled=True)]
    all_to_all x1 -> x2, starting transfers between devices: 45.1 us -> 10.3 us  [exchange(): return lax.all_to_all(blocks, axis, 0, 0, tiled=True)]
    unnamed x1 -> x0, blocking collectives: 27.3 us -> none
    all_to_all x1 -> x2, waiting for transfers between devices: 1.75 us -> 23.7 us  [exchange(): return lax.all_to_all(blocks, axis, 0, 0, tiled=True)]
    unnamed x26 -> x15, local copies, waits for them, and re-layouts: 11.2 us -> 1.89 us
  transfers between devices with their start and end apart: 3 -> 4, of which waited for: 3 -> 4; matrix products, arithmetic and copies ran while one was open for 2% -> 2% of each run, Pallas kernels for 0% -> 0%
where the time goes in v1:
time: 135 us
  starting transfers between devices  61.6 us (46%)
  blocking collectives  35.2 us (26%)
  waiting for transfers between devices  24.6 us (18%)
  local copies, waits for them, and re-layouts  5.97 us (4%)
  matrix products  5.58 us (4%)
    ppermute x2, starting transfers between devices, swap_cores(): return lax.ppermute(shard, 'col', [(0, 1), (1, 0)])  51.4 us
    all_to_all x2, blocking collectives, exchange(): return lax.all_to_all(blocks, axis, 0, 0, tiled=True)  35.2 us
    all_to_all x2, waiting for transfers between devices, exchange(): return lax.all_to_all(blocks, axis, 0, 0, tiled=True)  23.7 us
    all_to_all x2, starting transfers between devices, exchange(): return lax.all_to_all(blocks, axis, 0, 0, tiled=True)  10.3 us
    dot_general x5, matrix products, matmul(): jnp.dot(left, right, preferred_element_type=jnp.float32, precision=lax.Pr...  4.31 us
  transfers between devices with their start and end apart: 4, of which 4 were waited for; matrix products, arithmetic and copies ran while one was open for 2% of the time, Pallas kernels for 0%

profile of v1, /device:TPU:65, one launch (start us, length us, event | category | flops | bytes accessed | tf_op | source)
XLA Modules:
  0.0 134.7 jit_solution(9525141958632940281)
XLA Ops:
  0.6 0.0 copy-start
  0.6 0.0 copy-start.2
  0.7 0.9 copy-done
  1.6 1.3 fusion.11
  2.9 0.0 copy-done.2
  2.9 0.0 copy-start.1
  2.9 1.4 %convolution_add_fusion.2 = f32[256,256]{1,0:T(8,128)S(1)} fusion(f32[256,256]{1,0:T(8,128)S(1)} %fusion.11, f32[256,256]{1,0:T(8,128)} %param.9, f32[768,256]{1,0:T(8,128)S(1)} %copy-done.2), kind=kOutput, calls=%fused_computation.2 | convolution fusion | flops 201392128 | bytes 1048576 | tf_op jit(solution)/shard_map/dot_general | solution.py:25
  4.3 0.0 copy-done.1
  4.3 0.4 convolution_add_fusion.3
  4.7 0.0 copy-start.3
  4.7 0.1 pad_maximum_fusion
  4.8 43.5 %collective-permute-start = (f32[256,512]{1,0:T(8,128)S(1)}, f32[256,512]{1,0:T(8,128)S(1)}, u32[]{:S(2)}, u32[]{:S(2)}) collective-permute-start(f32[256,512]{1,0:T(8,128)S(1)} %pad_maximum_fusion), channel_id=1, source_target_pairs={{0,1},{1,0},{2,3},{3,2},{4,5},{5,4},{6,7},{7,6},{8,9},{9,8},{10,11... | collective-permute-start | bytes 1572872 | tf_op jit(solution)/shard_map/ppermute | solution.py:21
  48.3 0.0 copy-done.3
  48.4 0.4 reshape.68
  48.7 0.6 fusion.8
  49.4 0.5 collective-permute-done
  49.8 0.6 convolution_add_fusion.1
  50.4 20.4 %all_to_all.20 = f32[8,32,512]{2,1,0:T(8,128)S(1)} all-to-all(f32[8,32,512]{2,1,0:T(8,128)S(1)} %bitcast.35), channel_id=1, replica_groups=mesh['chan'=2,'row_0'=16,'row_1'=8,'col'=2] {'row_1'}, dimensions={0} | all-to-all | bytes 1048576 | tf_op jit(solution)/shard_map/all_to_all | solution.py:13
  70.9 0.6 reshape.70
  71.5 6.5 %all-to-all-start.1 = ((f32[16,8,128]{2,1,0:T(8,128)}), f32[16,8,128]{2,1,0:T(8,128)S(1)}, u32[]{:S(2)}, u32[]{:S(2)}) async-start(f32[16,8,128]{2,1,0:T(8,128)} %reshape.70), calls=%async_computation.1 | async-start | bytes 131072 | tf_op jit(solution)/shard_map/all_to_all | solution.py:13
  78.1 0.0 copy-start.4
  78.1 11.3 %all-to-all-done.1 = f32[16,8,128]{2,1,0:T(8,128)S(1)} async-done(((f32[16,8,128]{2,1,0:T(8,128)}), f32[16,8,128]{2,1,0:T(8,128)S(1)}, u32[]{:S(2)}, u32[]{:S(2)}) %all-to-all-start.1) | async-done | bytes 65568 | tf_op jit(solution)/shard_map/all_to_all | solution.py:13
  89.4 0.0 copy-done.4
  89.5 0.0 copy-start.5
  89.5 0.7 copy-done.5
  90.2 14.8 %all_to_all.21 = f32[16,10,128]{2,1,0:T(8,128)S(1)} all-to-all(f32[16,10,128]{2,1,0:T(8,128)S(1)} %broadcast_in_dim.4), channel_id=1, replica_groups=mesh['chan'=2,'row_0'=16,'row_1'=8,'col'=2] {'row_0'}, dimensions={0} | all-to-all | bytes 163840 | tf_op jit(solution)/shard_map/all_to_all | solution.py:13
  105.0 0.8 broadcast_in_dim.5
  105.9 3.7 %all-to-all-start.3 = ((f32[8,130,128]{2,1,0:T(8,128)}), f32[8,130,128]{2,1,0:T(8,128)S(1)}, u32[]{:S(2)}, u32[]{:S(2)}) async-start(f32[8,130,128]{2,1,0:T(8,128)} %broadcast_in_dim.5), calls=%async_computation.3 | async-start | bytes 1114112 | tf_op jit(solution)/shard_map/all_to_all | solution.py:13
  109.6 0.6 slice.81
  110.2 12.4 %all-to-all-done.3 = f32[8,130,128]{2,1,0:T(8,128)S(1)} async-done(((f32[8,130,128]{2,1,0:T(8,128)}), f32[8,130,128]{2,1,0:T(8,128)S(1)}, u32[]{:S(2)}, u32[]{:S(2)}) %all-to-all-start.3) | async-done | bytes 532512 | tf_op jit(solution)/shard_map/all_to_all | solution.py:13
  122.6 0.1 copy.25
  122.7 7.9 %collective-permute-start.1 = (f32[8,130,128]{2,0,1:T(8,128)S(1)}, f32[8,130,128]{2,0,1:T(8,128)S(1)}, u32[]{:S(2)}, u32[]{:S(2)}) collective-permute-start(f32[8,130,128]{2,0,1:T(8,128)S(1)} %copy.25), channel_id=1, source_target_pairs={{0,1},{1,0},{2,3},{3,2},{4,5},{5,4},{6,7},{7,6},{8,9},{9,8},{10,11... | collective-permute-start | bytes 1597448 | tf_op jit(solution)/shard_map/ppermute | solution.py:21
  130.6 0.1 slice_bitcast_fusion
  130.8 0.1 reshape_squeeze.12
  130.9 0.1 reshape_squeeze.13
  131.1 0.6 fusion
  131.7 0.4 collective-permute-done.1
  132.1 0.6 broadcast_multiply_fusion
  132.8 0.1 copy.32
  132.9 0.1 reshape_squeeze.14
  133.0 0.1 copy.33
  133.1 0.1 reshape_squeeze.15
  133.2 0.6 convolution_add_fusion
  133.9 0.8 fusion.18
  (19 shorter events, 0.4 us)
Async XLA Ops:
  0.6 1.0 copy-start
  0.6 2.3 %copy-start.2 = (f32[768,256]{1,0:T(8,128)S(1)}, f32[768,256]{1,0:T(8,128)}, u32[]{:S(2)}) copy-start(f32[768,256]{1,0:T(8,128)} %param.11) | copy-start | bytes 2359300
  2.9 1.4 %copy-start.1 = (f32[256,256]{1,0:T(8,128)S(1)}, f32[256,256]{1,0:T(8,128)}, u32[]{:S(2)}) copy-start(f32[256,256]{1,0:T(8,128)} %param.7) | copy-start | bytes 786436
  4.7 43.6 %copy-start.3 = (f32[128,1,2,512]{3,2,1,0:T(2,128)S(1)}, f32[128,1,2,512]{3,2,1,0:T(2,128)}, u32[]{:S(2)}) copy-start(f32[128,1,2,512]{3,2,1,0:T(2,128)} %param.6) | copy-start | bytes 1572868
  4.8 45.0 %collective-permute-start = (f32[256,512]{1,0:T(8,128)S(1)}, f32[256,512]{1,0:T(8,128)S(1)}, u32[]{:S(2)}, u32[]{:S(2)}) collective-permute-start(f32[256,512]{1,0:T(8,128)S(1)} %pad_maximum_fusion), channel_id=1, source_target_pairs={{0,1},{1,0},{2,3},{3,2},{4,5},{5,4},{6,7},{7,6},{8,9},{9,8},{10,11... | collective-permute-start | bytes 1572872 | tf_op jit(solution)/shard_map/ppermute | solution.py:21
  71.5 17.9 %all-to-all-start.1 = ((f32[16,8,128]{2,1,0:T(8,128)}), f32[16,8,128]{2,1,0:T(8,128)S(1)}, u32[]{:S(2)}, u32[]{:S(2)}) async-start(f32[16,8,128]{2,1,0:T(8,128)} %reshape.70), calls=%async_computation.1 | async-start | bytes 131072 | tf_op jit(solution)/shard_map/all_to_all | solution.py:13
  78.1 11.4 %copy-start.4 = (f32[2,256]{1,0:T(2,128)}, f32[2,256]{1,0:T(2,128)S(1)}, u32[]{:S(2)}) copy-start(f32[2,256]{1,0:T(2,128)S(1)} %slice.80) | copy-start | bytes 6148
  89.5 0.7 copy-start.5
  105.9 16.7 %all-to-all-start.3 = ((f32[8,130,128]{2,1,0:T(8,128)}), f32[8,130,128]{2,1,0:T(8,128)S(1)}, u32[]{:S(2)}, u32[]{:S(2)}) async-start(f32[8,130,128]{2,1,0:T(8,128)} %broadcast_in_dim.5), calls=%async_computation.3 | async-start | bytes 1114112 | tf_op jit(solution)/shard_map/all_to_all | solution.py:13
  122.7 9.4 %collective-permute-start.1 = (f32[8,130,128]{2,0,1:T(8,128)S(1)}, f32[8,130,128]{2,0,1:T(8,128)S(1)}, u32[]{:S(2)}, u32[]{:S(2)}) collective-permute-start(f32[8,130,128]{2,0,1:T(8,128)S(1)} %copy.25), channel_id=1, source_target_pairs={{0,1},{1,0},{2,3},{3,2},{4,5},{5,4},{6,7},{7,6},{8,9},{9,8},{10,11... | collective-permute-start | bytes 1597448 | tf_op jit(solution)/shard_map/ppermute | solution.py:21

commit v2 on v1

v2 whole, which is shorter than its diff:
```python
import functools

import jax
import jax.numpy as jnp
from jax import lax
from jax.experimental import pallas as pl
from jax.experimental.pallas import tpu as pltpu
from jax.sharding import Mesh
from jax.sharding import PartitionSpec as P


ROW = ("row_0", "row_1")
CHAN_ROW_COL = ("chan", "row_0", "row_1", "col")
LANES = 128
SUBLANES = 8
MIB = 2**20
FILLER_FLOPS = 10**9
F32 = jnp.float32


def shape(*dims):
    return jax.ShapeDtypeStruct(dims, F32)


def exchange(blocks, axis):
    return lax.all_to_all(blocks, axis, 0, 0, tiled=True)


def swap_cores(shard):
    return lax.ppermute(shard, "col", [(0, 1), (1, 0)])


def matmul(left, right):
    return jnp.dot(left, right, preferred_element_type=F32, precision=lax.Precision.HIGHEST)


def call(kernel, out_shape, *args, in_spaces=None, scratch=(), flops=None, vmem=8):
    spaces = in_spaces or [pltpu.VMEM] * len(args)
    resident = pl.BlockSpec(memory_space=pltpu.VMEM)
    return pl.pallas_call(
        kernel,
        in_specs=[pl.BlockSpec(memory_space=space) for space in spaces],
        out_specs=jax.tree.map(lambda _: resident, out_shape),
        out_shape=out_shape,
        scratch_shapes=scratch,
        compiler_params=pltpu.CompilerParams(vmem_limit_bytes=vmem * MIB),
        cost_estimate=flops and pl.CostEstimate(flops=flops, transcendentals=0, bytes_accessed=0),
    )(*args)


def padded(count):
    return -(-count // SUBLANES) * SUBLANES


def partial_kernel(core, tile, other, part, own, ritz, out, scaled, block):
    n_x = out.shape[0]
    length = other.shape[0]
    per_x = part.shape[0] // n_x
    n_blocks = part.shape[1] // LANES
    n_rows, width = block.shape
    block[...] = own[:n_rows, width:]
    for b in range(width // LANES):
        at = slice(b * LANES, (b + 1) * LANES)
        scaled[b * n_rows : (b + 1) * n_rows] = own[:n_rows, at] * ritz[:, at]

    def finish(first):
        total = part[...] + matmul(tile[:, first : first + length], other[...])
        for i in range(n_x):
            for b in range(n_blocks):
                out[i, b * per_x : (b + 1) * per_x] = total[
                    i * per_x : (i + 1) * per_x, b * LANES : (b + 1) * LANES
                ]
            for b in range(width // LANES):
                first = n_blocks * per_x + b * n_rows
                lane = width + b * LANES
                out[i, first : first + n_rows] = own[:n_rows, lane : lane + LANES]
            last = n_blocks * per_x + n_rows * (width // LANES)
            if last < out.shape[1]:
                out[i, last:] = jnp.zeros((out.shape[1] - last, LANES), F32)

    @pl.when(core[0] == 0)
    def _():
        finish(length)

    @pl.when(core[0] != 0)
    def _():
        finish(0)


def sum_x_kernel(by_x, out, total, *, n_rows, n_blocks):
    n_x = by_x.shape[0]
    n_z = out.shape[0]
    per_block = n_z * n_rows
    n_sum = 2 * n_blocks * per_block
    running = by_x[0, :n_sum]
    for i in range(1, n_x):
        running = running + by_x[i, :n_sum]
    total[...] = running
    head = 2 * n_blocks * n_rows
    for b in range(n_blocks):
        for i in range(n_x):
            first = head + (b * n_x + i) * n_rows
            out[0, first : first + n_rows] = by_x[
                i, n_sum + b * n_rows : n_sum + (b + 1) * n_rows
            ]
    for z in range(n_z):
        if z:
            out[z, head:] = out[0, head:]
        for b in range(2 * n_blocks):
            first = b * per_block + z * n_rows
            out[z, b * n_rows : (b + 1) * n_rows] = total[first : first + n_rows]


def residual_kernel(by_z, scaled, residual, out, mine, *, n_rows, n_blocks):
    n_lines = n_blocks * n_rows
    running = by_z[0, : 2 * n_lines]
    for z in range(1, by_z.shape[0]):
        running = running + by_z[z, : 2 * n_lines]
    rest = running[:n_lines] - scaled[...]
    residual[...] = rest
    squares = rest * rest
    mine[...] = jnp.zeros(mine.shape, F32)
    mine[:n_lines] = running[n_lines:]
    for b in range(n_blocks):
        mine[n_lines + b : n_lines + b + 1] = jnp.sum(
            squares[b * n_rows : (b + 1) * n_rows], axis=0, keepdims=True
        )
    for z in range(out.shape[0]):
        out[z] = mine[...]


def window_kernel(by_z, window, *, n_x, n_rows, n_blocks):
    n_z = by_z.shape[0]
    head = 2 * n_blocks * n_rows
    for z in range(n_z):
        for b in range(n_blocks):
            for i in range(n_x):
                first = head + (b * n_x + i) * n_rows
                to = (i * n_z + z) * n_rows
                window[to : to + n_rows, b * LANES : (b + 1) * LANES] = by_z[
                    z, first : first + n_rows
                ]


def metric_kernel(own, other, own_t, other_t, metric):
    own_t[...] = own[...].T
    other_t[...] = other[...].T
    metric[...] = matmul(own_t[...], own[...]) + matmul(other_t[...], other[...])


def gather_kernel(by_z, out, *, n_rows, n_blocks):
    n_z = by_z.shape[0]
    n_lines = n_blocks * n_rows
    for z in range(n_z):
        for b in range(n_blocks):
            first = (b * n_z + z) * n_rows
            out[0, first : first + n_rows] = by_z[z, b * n_rows : (b + 1) * n_rows]
    running = by_z[0, n_lines : n_lines + n_blocks]
    for z in range(1, n_z):
        running = running + by_z[z, n_lines : n_lines + n_blocks]
    last = n_z * n_lines
    out[0, last:] = jnp.zeros((out.shape[1] - last, LANES), F32)
    out[0, last : last + n_blocks] = running
    for i in range(1, out.shape[0]):
        out[i] = out[0]


def matrix_of(lines, scratch, n_blocks, per_block):
    for i in range(lines.shape[0]):
        for b in range(n_blocks):
            scratch[i * per_block : (i + 1) * per_block, b * LANES : (b + 1) * LANES] = lines[
                i, b * per_block : (b + 1) * per_block
            ]


def square_of(lines, n_gathered, n_blocks):
    running = lines[0, n_gathered : n_gathered + n_blocks]
    for i in range(1, lines.shape[0]):
        running = running + lines[i, n_gathered : n_gathered + n_blocks]
    return running


def own_kernel(lines, window_t, ritz, scratch, *, n_blocks, per_block):
    matrix_of(lines, scratch, n_blocks, per_block)
    ritz[...] = matmul(window_t[...], scratch[...])


def final_kernel(
    part, lines, own_lines, window_t, residual, ritz, correction, scratch, *, n_blocks, per_block, total
):
    matrix_of(lines, scratch, n_blocks, per_block)
    ritz[...] = part[...] + matmul(window_t[...], scratch[...])
    n_rows = correction.shape[0]
    n_gathered = n_blocks * per_block
    squares = square_of(own_lines, n_gathered, n_blocks) + square_of(lines, n_gathered, n_blocks)
    scale = lax.rsqrt(squares / total + 1e-06)
    for b in range(n_blocks):
        correction[:, b * LANES : (b + 1) * LANES] = (
            residual[b * n_rows : (b + 1) * n_rows] * scale[b : b + 1]
        )


def step(
    hamiltonian_rows, current_block, correction_block, previous_block, ritz_values, mixing_coeffs
):
    n_z, n_x, n_c = (lax.axis_size(a) for a in ("row_0", "row_1", "col"))
    own_len, width = current_block.shape
    n_rows = hamiltonian_rows.shape[2]
    n_blocks = width // LANES
    window_total = n_rows * n_z * n_x * n_c
    per_block = n_z * n_rows
    n_lines = n_blocks * n_rows
    core = lax.axis_index("col")
    sizes = dict(n_rows=n_rows, n_blocks=n_blocks)

    direction = matmul(correction_block, mixing_coeffs[width : 2 * width]) + matmul(
        previous_block, mixing_coeffs[2 * width :]
    )
    mixed = matmul(current_block, mixing_coeffs[:width]) + direction
    own = jnp.concatenate([current_block, mixed], axis=1)
    next_direction = direction[:n_rows]

    other = swap_cores(own)
    tile = hamiltonian_rows.reshape(n_z, n_x, n_rows, n_c * own_len)
    tile = tile.transpose(1, 0, 2, 3).reshape(n_x * per_block, n_c * own_len)
    part = matmul(lax.dynamic_slice_in_dim(tile, core * own_len, own_len, 1), own)
    n_sum = 2 * n_blocks * per_block
    partial, scaled, next_block = call(
        partial_kernel,
        (
            shape(n_x, n_sum + padded(n_lines), LANES),
            shape(n_lines, LANES),
            shape(n_rows, width),
        ),
        core.reshape(1),
        tile,
        other,
        part,
        own,
        ritz_values[None],
        in_spaces=[pltpu.SMEM] + [pltpu.VMEM] * 5,
    )

    by_x = exchange(partial, "row_1")
    slots = call(
        functools.partial(sum_x_kernel, **sizes),
        shape(n_z, 2 * n_lines + n_x * n_lines, LANES),
        by_x,
        scratch=[pltpu.VMEM((n_sum, LANES), F32)],
    )
    by_z = exchange(slots, "row_0")
    residual, mine = call(
        functools.partial(residual_kernel, **sizes),
        (shape(n_lines, LANES), shape(n_z, padded(n_lines + n_blocks), LANES)),
        by_z,
        scaled,
        scratch=[pltpu.VMEM((padded(n_lines + n_blocks), LANES), F32)],
    )

    y_z = exchange(mine, "row_0")
    window = call(
        functools.partial(window_kernel, n_x=n_x, **sizes),
        shape(n_x * per_block, width),
        by_z,
        flops=FILLER_FLOPS,
    )
    own_t, other_t, metric_matrix = call(
        metric_kernel,
        (
            shape(width, n_x * per_block),
            shape(width, n_x * per_block),
            shape(width, width),
        ),
        window,
        swap_cores(window),
        flops=FILLER_FLOPS,
    )
    copies = call(
        functools.partial(gather_kernel, **sizes),
        shape(n_x, n_z * n_lines + padded(n_blocks), LANES),
        y_z,
    )
    y_x = exchange(copies, "row_1")
    other_y = swap_cores(y_x)
    scratch = [pltpu.VMEM((n_x * per_block, width), F32)]
    ritz_part = call(
        functools.partial(own_kernel, n_blocks=n_blocks, per_block=per_block),
        shape(width, width),
        y_x,
        own_t,
        scratch=scratch,
    )
    ritz_matrix, next_correction = call(
        functools.partial(
            final_kernel, n_blocks=n_blocks, per_block=per_block, total=window_total
        ),
        (shape(width, width), shape(n_rows, width)),
        ritz_part,
        other_y,
        y_x,
        other_t,
        residual,
        scratch=scratch,
    )
    return (next_block, next_direction, next_correction, ritz_matrix, metric_matrix)


def solution(mesh):
    finer = Mesh(
        mesh.devices.reshape(mesh.shape["chan"], 16, 8, mesh.shape["col"]),
        ("chan", "row_0", "row_1", "col"),
    )
    in_specs = (
        P("chan", "col", None, ROW),
        P(CHAN_ROW_COL, None),
        P(CHAN_ROW_COL, None),
        P(CHAN_ROW_COL, None),
        P("chan"),
        P("chan", None),
    )
    out_specs = (
        P(CHAN_ROW_COL, None),
        P(CHAN_ROW_COL, None),
        P(CHAN_ROW_COL, None),
        P("chan", None),
        P("chan", None),
    )
    return jax.shard_map(step, mesh=finer, in_specs=in_specs, out_specs=out_specs, check_vma=False)
```

time: 135 us -> 141 us (1.044)
  blocking collectives: 35.2 us -> 65.5 us
  waiting for transfers between devices: 24.6 us -> 5.52 us
  Pallas kernels: 0 us -> 5.08 us
  starting transfers between devices: 61.6 us -> 57.2 us
  local copies, waits for them, and re-layouts: 5.97 us -> 2.61 us
  matrix products: 5.58 us -> 3.7 us
    all_to_all x2 -> x3, blocking collectives: 35.2 us -> 65.5 us  [exchange(): return lax.all_to_all(blocks, axis, 0, 0, tiled=True)]
    all_to_all x2 -> x1, waiting for transfers between devices: 23.7 us -> 5.06 us  [exchange(): return lax.all_to_all(blocks, axis, 0, 0, tiled=True)]
    all_to_all x2 -> x1, starting transfers between devices: 10.3 us -> 3.63 us  [exchange(): return lax.all_to_all(blocks, axis, 0, 0, tiled=True)]
    pallas_call x0 -> x8, Pallas kernels: none -> 5.08 us  [call(): pl.pallas_call(kernel, in_specs=[pl.BlockSpec(memory_space=space) for spa...]
    ppermute x2 -> x3, starting transfers between devices: 51.4 us -> 53.5 us  [swap_cores(): return lax.ppermute(shard, 'col', [(0, 1), (1, 0)])]
    dot_general x7 -> x4, matrix products: 5.58 us -> 3.7 us  [matmul(): jnp.dot(left, right, preferred_element_type=F32, precision=lax.Precision....]
  transfers between devices with their start and end apart: 4 -> 4, of which waited for: 4 -> 2; matrix products, arithmetic and copies ran while one was open for 2% -> 1% of each run, Pallas kernels for 0% -> 1%
where the time goes in v2:
time: 141 us; the launch traced here: 140 us
  blocking collectives  65.5 us (46%)
  starting transfers between devices  57.2 us (41%)
  waiting for transfers between devices  5.52 us (4%)
  Pallas kernels  5.08 us (4%)
  matrix products  3.7 us (3%)
  local copies, waits for them, and re-layouts  2.61 us (2%)
    all_to_all x3, blocking collectives, exchange(): return lax.all_to_all(blocks, axis, 0, 0, tiled=True)  65.5 us
    ppermute x3, starting transfers between devices, swap_cores(): return lax.ppermute(shard, 'col', [(0, 1), (1, 0)])  53.5 us
    pallas_call x8, Pallas kernels, call(): pl.pallas_call(kernel, in_specs=[pl.BlockSpec(memory_space=space) for spa...  5.08 us
    all_to_all x1, waiting for transfers between devices, exchange(): return lax.all_to_all(blocks, axis, 0, 0, tiled=True)  5.06 us
    dot_general x4, matrix products, matmul(): jnp.dot(left, right, preferred_element_type=F32, precision=lax.Precision....  3.7 us
    all_to_all x1, starting transfers between devices, exchange(): return lax.all_to_all(blocks, axis, 0, 0, tiled=True)  3.63 us
  transfers between devices with their start and end apart: 4, of which 2 were waited for; matrix products, arithmetic and copies ran while one was open for 1% of the time, Pallas kernels for 1%

profile of v2, /device:TPU:65, one launch (start us, length us, event | category | flops | bytes accessed | tf_op | source)
XLA Modules:
  0.0 140.5 jit_solution(18344478598773186961)
XLA Ops:
  0.6 0.0 copy-start
  0.6 0.0 copy-start.3
  0.7 0.9 copy-done
  1.6 1.3 fusion.3
  2.9 0.0 copy-done.3
  2.9 0.0 copy-start.2
  2.9 1.4 convolution_add_fusion
  4.3 0.0 copy-done.2
  4.3 0.4 convolution_add_fusion.1
  4.7 0.0 copy-start.4
  4.7 0.1 pad_maximum_fusion.own
  4.8 43.5 %collective-permute-start = (f32[256,512]{1,0:T(8,128)S(1)}, f32[256,512]{1,0:T(8,128)S(1)}, u32[]{:S(2)}, u32[]{:S(2)}) collective-permute-start(f32[256,512]{1,0:T(8,128)S(1)} %pad_maximum_fusion.own), channel_id=1, source_target_pairs={{0,1},{1,0},{2,3},{3,2},{4,5},{5,4},{6,7},{7,6},{8,9},{9,8},{10,11... | collective-permute-start | bytes 1572872 | tf_op jit(solution)/shard_map/ppermute | solution.py:30
  48.3 0.0 copy-done.4
  48.4 0.4 reshape.21.tile
  48.7 0.6 fusion.part
  49.4 0.5 collective-permute-done.other
  49.8 0.0 copy-start.1
  49.8 0.7 copy-done.1
  50.5 1.2 shard_map.101
  51.7 20.6 %all_to_all.20.by_x = f32[8,136,128]{2,1,0:T(8,128)S(1)} all-to-all(f32[8,136,128]{2,1,0:T(8,128)S(1)} %get-tuple-element.16), channel_id=1, replica_groups=mesh['chan'=2,'row_0'=16,'row_1'=8,'col'=2] {'row_1'}, dimensions={0} | all-to-all | bytes 1114112 | tf_op jit(solution)/shard_map/all_to_all | solution.py:26
  72.3 0.1 shard_map.102
  72.4 21.0 %all_to_all.21.by_z = f32[16,40,128]{2,1,0:T(8,128)S(1)} all-to-all(f32[16,40,128]{2,1,0:T(8,128)S(1)} %shard_map.102), channel_id=1, replica_groups=mesh['chan'=2,'row_0'=16,'row_1'=8,'col'=2] {'row_0'}, dimensions={0} | all-to-all | bytes 655360 | tf_op jit(solution)/shard_map/all_to_all | solution.py:26
  93.5 23.9 %all_to_all.22.by_z = f32[16,8,128]{2,1,0:T(8,128)S(1)} all-to-all(f32[16,8,128]{2,1,0:T(8,128)S(1)} %get-tuple-element.18), channel_id=1, replica_groups=mesh['chan'=2,'row_0'=16,'row_1'=8,'col'=2] {'row_0'}, dimensions={0} | all-to-all | bytes 131072 | tf_op jit(solution)/shard_map/all_to_all | solution.py:26
  117.4 0.8 shard_map.104
  118.1 3.6 %all-to-all-start.3 = ((f32[8,72,128]{2,1,0:T(8,128)}), f32[8,72,128]{2,1,0:T(8,128)S(1)}, u32[]{:S(2)}, u32[]{:S(2)}) async-start(f32[8,72,128]{2,1,0:T(8,128)} %shard_map.104), calls=%async_computation.3 | async-start | bytes 589824 | tf_op jit(solution)/shard_map/all_to_all | solution.py:26
  121.7 0.1 shard_map.105.own
  121.9 4.4 %collective-permute-start.1 = (f32[256,256]{1,0:T(8,128)S(1)}, f32[256,256]{1,0:T(8,128)S(1)}, u32[]{:S(2)}, u32[]{:S(2)}) collective-permute-start(f32[256,256]{1,0:T(8,128)S(1)} %shard_map.105.own), channel_id=1, source_target_pairs={{0,1},{1,0},{2,3},{3,2},{4,5},{5,4},{6,7},{7,6},{8,9},{9,8},{10,11... | collective-permute-start | bytes 786440 | tf_op jit(solution)/shard_map/ppermute | solution.py:30
  126.2 5.1 %all-to-all-done.3.lines.own_lines = f32[8,72,128]{2,1,0:T(8,128)S(1)} async-done(((f32[8,72,128]{2,1,0:T(8,128)}), f32[8,72,128]{2,1,0:T(8,128)S(1)}, u32[]{:S(2)}, u32[]{:S(2)}) %all-to-all-start.3) | async-done | bytes 294944 | tf_op jit(solution)/shard_map/all_to_all | solution.py:26
  131.3 5.6 %collective-permute-start.2 = (f32[8,72,128]{2,1,0:T(8,128)S(1)}, f32[8,72,128]{2,1,0:T(8,128)S(1)}, u32[]{:S(2)}, u32[]{:S(2)}) collective-permute-start(f32[8,72,128]{2,1,0:T(8,128)S(1)} %all-to-all-done.3.lines.own_lines), channel_id=1, source_target_pairs={{0,1},{1,0},{2,3},{3,2},{4,5},{5,4},{6,7},{7,6},{8,9},{9,8},{10,11... | collective-permute-start | bytes 884744 | tf_op jit(solution)/shard_map/ppermute | solution.py:30
  137.0 0.6 slice.16
  137.5 0.0 collective-permute-done.1.other
  137.5 1.4 %shard_map.106 = (f32[256,256]{1,0:T(8,128)S(1)}, f32[256,256]{1,0:T(8,128)S(1)}, f32[256,256]{1,0:T(8,128)}) custom-call(f32[256,256]{1,0:T(8,128)S(1)} %shard_map.105.own, f32[256,256]{1,0:T(8,128)S(1)} %collective-permute-done.1.other), custom_call_target="tpu_custom_call" | custom-call | flops 1000000000 | tf_op jit(solution)/shard_map/pallas_call | solution.py:40
  139.0 0.4 shard_map.107.part
  139.4 0.0 collective-permute-done.2.lines
  139.4 1.1 shard_map.108
  (2 shorter events, 0.1 us)
Async XLA Ops:
  0.6 1.0 copy-start
  0.6 2.3 %copy-start.3 = (f32[768,256]{1,0:T(8,128)S(1)}, f32[768,256]{1,0:T(8,128)}, u32[]{:S(2)}) copy-start(f32[768,256]{1,0:T(8,128)} %param.11) | copy-start | bytes 2359300
  2.9 1.4 copy-start.2
  4.7 43.6 %copy-start.4 = (f32[128,1,2,512]{3,2,1,0:T(2,128)S(1)}, f32[128,1,2,512]{3,2,1,0:T(2,128)}, u32[]{:S(2)}) copy-start(f32[128,1,2,512]{3,2,1,0:T(2,128)} %param.6) | copy-start | bytes 1572868
  4.8 45.0 %collective-permute-start = (f32[256,512]{1,0:T(8,128)S(1)}, f32[256,512]{1,0:T(8,128)S(1)}, u32[]{:S(2)}, u32[]{:S(2)}) collective-permute-start(f32[256,512]{1,0:T(8,128)S(1)} %pad_maximum_fusion.own), channel_id=1, source_target_pairs={{0,1},{1,0},{2,3},{3,2},{4,5},{5,4},{6,7},{7,6},{8,9},{9,8},{10,11... | collective-permute-start | bytes 1572872 | tf_op jit(solution)/shard_map/ppermute | solution.py:30
  49.8 0.7 copy-start.1
  118.1 13.2 %all-to-all-start.3 = ((f32[8,72,128]{2,1,0:T(8,128)}), f32[8,72,128]{2,1,0:T(8,128)S(1)}, u32[]{:S(2)}, u32[]{:S(2)}) async-start(f32[8,72,128]{2,1,0:T(8,128)} %shard_map.104), calls=%async_computation.3 | async-start | bytes 589824 | tf_op jit(solution)/shard_map/all_to_all | solution.py:26
  121.9 15.7 %collective-permute-start.1 = (f32[256,256]{1,0:T(8,128)S(1)}, f32[256,256]{1,0:T(8,128)S(1)}, u32[]{:S(2)}, u32[]{:S(2)}) collective-permute-start(f32[256,256]{1,0:T(8,128)S(1)} %shard_map.105.own), channel_id=1, source_target_pairs={{0,1},{1,0},{2,3},{3,2},{4,5},{5,4},{6,7},{7,6},{8,9},{9,8},{10,11... | collective-permute-start | bytes 786440 | tf_op jit(solution)/shard_map/ppermute | solution.py:30
  131.3 8.1 %collective-permute-start.2 = (f32[8,72,128]{2,1,0:T(8,128)S(1)}, f32[8,72,128]{2,1,0:T(8,128)S(1)}, u32[]{:S(2)}, u32[]{:S(2)}) collective-permute-start(f32[8,72,128]{2,1,0:T(8,128)S(1)} %all-to-all-done.3.lines.own_lines), channel_id=1, source_target_pairs={{0,1},{1,0},{2,3},{3,2},{4,5},{5,4},{6,7},{7,6},{8,9},{9,8},{10,11... | collective-permute-start | bytes 884744 | tf_op jit(solution)/shard_map/ppermute | solution.py:30

commit v3 on v2

v3 whole, which is shorter than its diff:
```python
import functools

import jax
import jax.numpy as jnp
from jax import lax
from jax.experimental import pallas as pl
from jax.experimental.pallas import tpu as pltpu
from jax.sharding import Mesh
from jax.sharding import PartitionSpec as P

ROW = ("row_0", "row_1")
CHAN_ROW_COL = ("chan", "row_0", "row_1", "col")
LANES = 128
SUBLANES = 8
VMEM_BYTES = 8 * 2**20
F32 = jnp.float32


def shape(*dims):
    return jax.ShapeDtypeStruct(dims, F32)


def exchange(blocks, axis):
    return lax.all_to_all(blocks, axis, 0, 0, tiled=True)


def swap_cores(shard):
    return lax.ppermute(shard, "col", [(0, 1), (1, 0)])


def matmul(left, right):
    return jnp.dot(left, right, preferred_element_type=F32, precision=lax.Precision.HIGHEST)


def call(kernel, name, out_shape, *args, in_spaces=None, scratch=()):
    spaces = in_spaces or [pltpu.VMEM] * len(args)
    resident = pl.BlockSpec(memory_space=pltpu.VMEM)
    return pl.pallas_call(
        kernel,
        in_specs=[pl.BlockSpec(memory_space=space) for space in spaces],
        out_specs=jax.tree.map(lambda _: resident, out_shape),
        out_shape=out_shape,
        scratch_shapes=scratch,
        compiler_params=pltpu.CompilerParams(vmem_limit_bytes=VMEM_BYTES),
        name=name,
    )(*args)


def padded(count):
    return -(-count // SUBLANES) * SUBLANES


def partial_kernel(core, tile, other, part, scaled, direction, out, scaled_lines, first_rows):
    n_x = out.shape[0]
    length = other.shape[0]
    per_x = part.shape[0] // n_x
    n_blocks = part.shape[1] // LANES
    n_rows, width = first_rows.shape
    first_rows[...] = direction[:n_rows]
    for b in range(width // LANES):
        at = slice(b * LANES, (b + 1) * LANES)
        scaled_lines[b * n_rows : (b + 1) * n_rows] = scaled[:, at]

    def finish(first):
        total = part[...] + matmul(tile[:, first : first + length], other[...])
        for i in range(n_x):
            for b in range(n_blocks):
                out[i, b * per_x : (b + 1) * per_x] = total[
                    i * per_x : (i + 1) * per_x, b * LANES : (b + 1) * LANES
                ]

    @pl.when(core[0] == 0)
    def _():
        finish(length)

    @pl.when(core[0] != 0)
    def _():
        finish(0)


def sum_x_kernel(by_x, own, out, block, lines, total, *, n_rows, n_blocks):
    n_x = by_x.shape[0]
    n_z = out.shape[0]
    running = by_x[0]
    for i in range(1, n_x):
        running = running + by_x[i]
    total[...] = running
    for z in range(n_z):
        for b in range(2 * n_blocks):
            first = (b * n_z + z) * n_rows
            out[z, b * n_rows : (b + 1) * n_rows] = total[first : first + n_rows]
    first = n_blocks * LANES
    block[...] = own[:n_rows, first:]
    for b in range(n_blocks):
        at = slice(first + b * LANES, first + (b + 1) * LANES)
        lines[b * n_rows : (b + 1) * n_rows] = own[:n_rows, at]


def residual_kernel(by_z, scaled, lines, residual, out, mine, *, n_rows, n_blocks):
    n_lines = n_blocks * n_rows
    running = by_z[0]
    for z in range(1, by_z.shape[0]):
        running = running + by_z[z]
    rest = running[:n_lines] - scaled[...]
    residual[...] = rest
    squares = rest * rest
    mine[...] = jnp.zeros(mine.shape, F32)
    mine[:n_lines] = running[n_lines:]
    mine[n_lines : 2 * n_lines] = lines[...]
    for b in range(n_blocks):
        at = slice(b * n_rows, (b + 1) * n_rows)
        mine[2 * n_lines + b : 2 * n_lines + b + 1] = jnp.sum(squares[at], axis=0, keepdims=True)
    for z in range(out.shape[0]):
        out[z] = mine[...]


def gather_kernel(by_z, out, *, n_rows, n_blocks):
    n_z = by_z.shape[0]
    n_lines = 2 * n_blocks * n_rows
    for z in range(n_z):
        for b in range(2 * n_blocks):
            first = (b * n_z + z) * n_rows
            out[0, first : first + n_rows] = by_z[z, b * n_rows : (b + 1) * n_rows]
    running = by_z[0, n_lines : n_lines + n_blocks]
    for z in range(1, n_z):
        running = running + by_z[z, n_lines : n_lines + n_blocks]
    last = n_z * n_lines
    out[0, last:] = jnp.zeros((out.shape[1] - last, LANES), F32)
    out[0, last : last + n_blocks] = running
    for i in range(1, out.shape[0]):
        out[i] = out[0]


def grams(lines, product, window, n_blocks, per_block):
    for i in range(lines.shape[0]):
        to = slice(i * per_block, (i + 1) * per_block)
        for b in range(n_blocks):
            at = slice(b * LANES, (b + 1) * LANES)
            product[to, at] = lines[i, b * per_block : (b + 1) * per_block]
            first = (n_blocks + b) * per_block
            window[to, at] = lines[i, first : first + per_block]
    turned = window[...].T
    return matmul(turned, product[...]), matmul(turned, window[...])


def square_of(lines, n_gathered, n_blocks):
    running = lines[0, n_gathered : n_gathered + n_blocks]
    for i in range(1, lines.shape[0]):
        running = running + lines[i, n_gathered : n_gathered + n_blocks]
    return running


def own_kernel(lines, ritz, metric, product, window, *, n_blocks, per_block):
    ritz[...], metric[...] = grams(lines, product, window, n_blocks, per_block)


def final_kernel(
    ritz_part, metric_part, lines, own_lines, residual, ritz, metric, correction, product, window,
    *, n_blocks, per_block, total
):
    other_ritz, other_metric = grams(lines, product, window, n_blocks, per_block)
    ritz[...] = ritz_part[...] + other_ritz
    metric[...] = metric_part[...] + other_metric
    n_rows = correction.shape[0]
    n_gathered = 2 * n_blocks * per_block
    squares = square_of(own_lines, n_gathered, n_blocks) + square_of(lines, n_gathered, n_blocks)
    scale = lax.rsqrt(squares / total + 1e-06)
    for b in range(n_blocks):
        correction[:, b * LANES : (b + 1) * LANES] = (
            residual[b * n_rows : (b + 1) * n_rows] * scale[b : b + 1]
        )


def on_device(
    hamiltonian_rows, current_block, correction_block, previous_block, ritz_values, mixing_coeffs
):
    n_z, n_x, n_c = (lax.axis_size(a) for a in ("row_0", "row_1", "col"))
    own_len, width = current_block.shape
    n_rows = hamiltonian_rows.shape[2]
    n_blocks = width // LANES
    window_total = n_rows * n_z * n_x * n_c
    per_block = n_z * n_rows
    n_lines = n_blocks * n_rows
    core = lax.axis_index("col")
    sizes = dict(n_rows=n_rows, n_blocks=n_blocks)

    direction = matmul(correction_block, mixing_coeffs[width : 2 * width]) + matmul(
        previous_block, mixing_coeffs[2 * width :]
    )
    mixed = matmul(current_block, mixing_coeffs[:width]) + direction
    own = jnp.concatenate([current_block, mixed], axis=1)
    scaled_rows = current_block[:n_rows] * ritz_values[None, :]

    other = swap_cores(own)
    tile = hamiltonian_rows.reshape(n_z, n_x, n_rows, n_c * own_len)
    tile = tile.transpose(1, 0, 2, 3).reshape(n_x * per_block, n_c * own_len)
    part = matmul(lax.dynamic_slice_in_dim(tile, core * own_len, own_len, 1), own)
    n_sum = 2 * n_blocks * per_block
    partial, scaled, next_direction = call(
        partial_kernel,
        "partial",
        (shape(n_x, n_sum, LANES), shape(n_lines, LANES), shape(n_rows, width)),
        core.reshape(1),
        tile,
        other,
        part,
        scaled_rows,
        direction,
        in_spaces=[pltpu.SMEM] + [pltpu.VMEM] * 5,
    )

    by_x = exchange(partial, "row_1")
    slots, next_block, block_lines = call(
        functools.partial(sum_x_kernel, **sizes),
        "sum_x",
        (shape(n_z, 2 * n_lines, LANES), shape(n_rows, width), shape(n_lines, LANES)),
        by_x,
        own,
        scratch=[pltpu.VMEM((n_sum, LANES), F32)],
    )
    by_z = exchange(slots, "row_0")
    n_mine = padded(2 * n_lines + n_blocks)
    residual, mine = call(
        functools.partial(residual_kernel, **sizes),
        "residual",
        (shape(n_lines, LANES), shape(n_z, n_mine, LANES)),
        by_z,
        scaled,
        block_lines,
        scratch=[pltpu.VMEM((n_mine, LANES), F32)],
    )

    copies = call(
        functools.partial(gather_kernel, **sizes),
        "gather",
        shape(n_x, 2 * n_z * n_lines + padded(n_blocks), LANES),
        exchange(mine, "row_0"),
    )
    lines = exchange(copies, "row_1")
    other_lines = swap_cores(lines)
    scratch = [pltpu.VMEM((n_x * per_block, width), F32)] * 2
    ritz_part, metric_part = call(
        functools.partial(own_kernel, n_blocks=n_blocks, per_block=per_block),
        "own_grams",
        (shape(width, width), shape(width, width)),
        lines,
        scratch=scratch,
    )
    ritz_matrix, metric_matrix, next_correction = call(
        functools.partial(
            final_kernel, n_blocks=n_blocks, per_block=per_block, total=window_total
        ),
        "final",
        (shape(width, width), shape(width, width), shape(n_rows, width)),
        ritz_part,
        metric_part,
        other_lines,
        lines,
        residual,
        scratch=scratch,
    )
    return (next_block, next_direction, next_correction, ritz_matrix, metric_matrix)


def solution(mesh):
    finer = Mesh(
        mesh.devices.reshape(mesh.shape["chan"], 16, 8, mesh.shape["col"]),
        ("chan", "row_0", "row_1", "col"),
    )
    in_specs = (
        P("chan", "col", None, ROW),
        P(CHAN_ROW_COL, None),
        P(CHAN_ROW_COL, None),
        P(CHAN_ROW_COL, None),
        P("chan"),
        P("chan", None),
    )
    out_specs = (
        P(CHAN_ROW_COL, None),
        P(CHAN_ROW_COL, None),
        P(CHAN_ROW_COL, None),
        P("chan", None),
        P("chan", None),
    )
    return jax.shard_map(
        on_device, mesh=finer, in_specs=in_specs, out_specs=out_specs, check_vma=False
    )
```

time: 141 us -> 132 us (0.936)
  starting transfers between devices: 57.2 us -> 51.1 us
  waiting for transfers between devices: 5.52 us -> 1.32 us
  blocking collectives: 65.5 us -> 68.8 us
    all_to_all x1 -> x0, waiting for transfers between devices: 5.06 us -> none  [exchange(): return lax.all_to_all(blocks, axis, 0, 0, tiled=True)]
    all_to_all x1 -> x0, starting transfers between devices: 3.63 us -> none  [exchange(): return lax.all_to_all(blocks, axis, 0, 0, tiled=True)]
    all_to_all x3 -> x4, blocking collectives: 65.5 us -> 68.8 us  [exchange(): return lax.all_to_all(blocks, axis, 0, 0, tiled=True)]
    ppermute x3 -> x2, starting transfers between devices: 53.5 us -> 51.1 us  [swap_cores(): return lax.ppermute(shard, 'col', [(0, 1), (1, 0)])]
    pallas_call x8 -> x6, Pallas kernels: 5.08 us -> 3.98 us  [call(): pl.pallas_call(kernel, in_specs=[pl.BlockSpec(memory_space=space) for spa...]
  transfers between devices with their start and end apart: 4 -> 2, of which waited for: 2 -> 2; matrix products, arithmetic and copies ran while one was open for 1% -> 1% of each run, Pallas kernels for 1% -> 0%
where the time goes in v3:
time: 132 us; the launch traced here: 131 us
  blocking collectives  68.8 us (52%)
  starting transfers between devices  51.1 us (39%)
  Pallas kernels  3.98 us (3%)
  matrix products  3.7 us (3%)
  local copies, waits for them, and re-layouts  1.4 us (1%)
  waiting for transfers between devices  1.32 us (1%)
    all_to_all x4, blocking collectives, exchange(): return lax.all_to_all(blocks, axis, 0, 0, tiled=True)  68.8 us
    ppermute x2, starting transfers between devices, swap_cores(): return lax.ppermute(shard, 'col', [(0, 1), (1, 0)])  51.1 us
    pallas_call x6, Pallas kernels, call(): pl.pallas_call(kernel, in_specs=[pl.BlockSpec(memory_space=space) for spa...  3.98 us
    dot_general x4, matrix products, matmul(): jnp.dot(left, right, preferred_element_type=F32, precision=lax.Precision....  3.7 us
  transfers between devices with their start and end apart: 2, of which 2 were waited for; matrix products, arithmetic and copies ran while one was open for 1% of the time, Pallas kernels for 0%

profile of v3, /device:TPU:65, one launch (start us, length us, event | category | flops | bytes accessed | tf_op | source)
XLA Modules:
  0.0 131.1 jit_solution(7680485717692284862)
XLA Ops:
  0.6 0.0 copy-start
  0.6 0.0 copy-start.2
  0.7 0.9 copy-done
  1.6 1.3 %fusion.3 = f32[256,256]{1,0:T(8,128)S(1)} fusion(f32[256,256]{1,0:T(8,128)S(1)} %copy-done, f32[768,256]{1,0:T(8,128)} %param.11), kind=kOutput, calls=%fused_computation.7 | convolution fusion | flops 201326592 | bytes 786432 | tf_op jit(solution)/shard_map/dot_general | solution.py:32
  2.9 0.0 copy-done.2
  2.9 0.0 copy-start.1
  2.9 1.4 %convolution_add_fusion.direction = f32[256,256]{1,0:T(8,128)S(1)} fusion(f32[256,256]{1,0:T(8,128)S(1)} %fusion.3, f32[256,256]{1,0:T(8,128)} %param.9, f32[768,256]{1,0:T(8,128)S(1)} %copy-done.2), kind=kOutput, calls=%fused_computation | convolution fusion | flops 201392128 | bytes 1048576 | tf_op jit(solution)/shard_map/dot_general | solution.py:32
  4.3 0.0 copy-done.1
  4.3 0.4 convolution_add_fusion.1
  4.7 0.0 copy-start.3
  4.7 0.1 pad_maximum_fusion.own
  4.8 43.5 %collective-permute-start = (f32[256,512]{1,0:T(8,128)S(1)}, f32[256,512]{1,0:T(8,128)S(1)}, u32[]{:S(2)}, u32[]{:S(2)}) collective-permute-start(f32[256,512]{1,0:T(8,128)S(1)} %pad_maximum_fusion.own), channel_id=1, source_target_pairs={{0,1},{1,0},{2,3},{3,2},{4,5},{5,4},{6,7},{7,6},{8,9},{9,8},{10,11... | collective-permute-start | bytes 1572872 | tf_op jit(solution)/shard_map/ppermute | solution.py:28
  48.3 0.0 copy-done.3
  48.4 0.4 reshape.22.tile
  48.7 0.0 copy-start.4
  48.8 0.6 fusion.part
  49.4 0.0 copy-done.4
  49.4 0.4 collective-permute-done.other
  49.8 1.2 partial.1
  51.0 20.4 %all_to_all.20.by_x = f32[8,128,128]{2,1,0:T(8,128)S(1)} all-to-all(f32[8,128,128]{2,1,0:T(8,128)S(1)} %get-tuple-element.18), channel_id=1, replica_groups=mesh['chan'=2,'row_0'=16,'row_1'=8,'col'=2] {'row_1'}, dimensions={0} | all-to-all | bytes 1048576 | tf_op jit(solution)/shard_map/all_to_all | solution.py:24
  71.4 0.6 sum_x.1
  72.0 17.7 %all_to_all.21.by_z = f32[16,8,128]{2,1,0:T(8,128)S(1)} all-to-all(f32[16,8,128]{2,1,0:T(8,128)S(1)} %get-tuple-element.21), channel_id=1, replica_groups=mesh['chan'=2,'row_0'=16,'row_1'=8,'col'=2] {'row_0'}, dimensions={0} | all-to-all | bytes 131072 | tf_op jit(solution)/shard_map/all_to_all | solution.py:24
  89.8 14.8 %all_to_all.22.by_z = f32[16,16,128]{2,1,0:T(8,128)S(1)} all-to-all(f32[16,16,128]{2,1,0:T(8,128)S(1)} %get-tuple-element.24), channel_id=1, replica_groups=mesh['chan'=2,'row_0'=16,'row_1'=8,'col'=2] {'row_0'}, dimensions={0} | all-to-all | bytes 262144 | tf_op jit(solution)/shard_map/all_to_all | solution.py:24
  104.6 0.1 gather.1
  104.6 15.9 %all_to_all.23.lines.own_lines = f32[8,136,128]{2,1,0:T(8,128)S(1)} all-to-all(f32[8,136,128]{2,1,0:T(8,128)S(1)} %gather.1), channel_id=1, replica_groups=mesh['chan'=2,'row_0'=16,'row_1'=8,'col'=2] {'row_1'}, dimensions={0} | all-to-all | bytes 1114112 | tf_op jit(solution)/shard_map/all_to_all | solution.py:24
  120.6 7.6 %collective-permute-start.1 = (f32[8,136,128]{2,1,0:T(8,128)S(1)}, f32[8,136,128]{2,1,0:T(8,128)S(1)}, u32[]{:S(2)}, u32[]{:S(2)}) collective-permute-start(f32[8,136,128]{2,1,0:T(8,128)S(1)} %all_to_all.23.lines.own_lines), channel_id=1, source_target_pairs={{0,1},{1,0},{2,3},{3,2},{4,5},{5,4},{6,7},{7,6},{8,9},{9,8},{10,11... | collective-permute-start | bytes 1671176 | tf_op jit(solution)/shard_map/ppermute | solution.py:28
  128.2 0.6 own_grams.1
  128.8 0.9 collective-permute-done.1.lines
  129.7 1.4 %final.1 = (f32[256,256]{1,0:T(8,128)}, f32[256,256]{1,0:T(8,128)}, f32[2,256]{1,0:T(2,128)}) custom-call(f32[256,256]{1,0:T(8,128)S(1)} %get-tuple-element.25.ritz_part, f32[256,256]{1,0:T(8,128)S(1)} %get-tuple-element.26.metric_part, f32[8,136,128]{2,1,0:T(8,128)S(1)} %collective-permute-done.1.lines, f32[8,136,128]{2,1,0:T(8,128)S(1)} %all_to_all.23.lines.own_lines, ...), custom_call_target="tpu_custom_call" | custom-call | tf_op jit(solution)/shard_map/final/pallas_call | solution.py:38
  (3 shorter events, 0.1 us)
Async XLA Ops:
  0.6 1.0 copy-start
  0.6 2.3 %copy-start.2 = (f32[768,256]{1,0:T(8,128)S(1)}, f32[768,256]{1,0:T(8,128)}, u32[]{:S(2)}) copy-start(f32[768,256]{1,0:T(8,128)} %param.11) | copy-start | bytes 2359300
  2.9 1.4 %copy-start.1 = (f32[256,256]{1,0:T(8,128)S(1)}, f32[256,256]{1,0:T(8,128)}, u32[]{:S(2)}) copy-start(f32[256,256]{1,0:T(8,128)} %param.7) | copy-start | bytes 786436
  4.7 43.6 %copy-start.3 = (f32[128,1,2,512]{3,2,1,0:T(2,128)S(1)}, f32[128,1,2,512]{3,2,1,0:T(2,128)}, u32[]{:S(2)}) copy-start(f32[128,1,2,512]{3,2,1,0:T(2,128)} %param.6) | copy-start | bytes 1572868
  4.8 45.0 %collective-permute-start = (f32[256,512]{1,0:T(8,128)S(1)}, f32[256,512]{1,0:T(8,128)S(1)}, u32[]{:S(2)}, u32[]{:S(2)}) collective-permute-start(f32[256,512]{1,0:T(8,128)S(1)} %pad_maximum_fusion.own), channel_id=1, source_target_pairs={{0,1},{1,0},{2,3},{3,2},{4,5},{5,4},{6,7},{7,6},{8,9},{9,8},{10,11... | collective-permute-start | bytes 1572872 | tf_op jit(solution)/shard_map/ppermute | solution.py:28
  48.7 0.7 copy-start.4
  120.6 9.2 %collective-permute-start.1 = (f32[8,136,128]{2,1,0:T(8,128)S(1)}, f32[8,136,128]{2,1,0:T(8,128)S(1)}, u32[]{:S(2)}, u32[]{:S(2)}) collective-permute-start(f32[8,136,128]{2,1,0:T(8,128)S(1)} %all_to_all.23.lines.own_lines), channel_id=1, source_target_pairs={{0,1},{1,0},{2,3},{3,2},{4,5},{5,4},{6,7},{7,6},{8,9},{9,8},{10,11... | collective-permute-start | bytes 1671176 | tf_op jit(solution)/shard_map/ppermute | solution.py:28

commit v4 on v3

--- a/solution.py
+++ b/solution.py
@@ -50,24 +50,28 @@
     return -(-count // SUBLANES) * SUBLANES
 
 
-def partial_kernel(core, tile, other, part, scaled, direction, out, scaled_lines, first_rows):
+def partial_kernel(
+    core, tile, other_x, other_b, part_x, part_b, scaled, mixed, out, scaled_lines, block_lines
+):
     n_x = out.shape[0]
-    length = other.shape[0]
-    per_x = part.shape[0] // n_x
-    n_blocks = part.shape[1] // LANES
-    n_rows, width = first_rows.shape
-    first_rows[...] = direction[:n_rows]
-    for b in range(width // LANES):
+    n_rows, width = scaled.shape
+    length = other_x.shape[0]
+    per_x = part_x.shape[0] // n_x
+    n_blocks = width // LANES
+    for b in range(n_blocks):
         at = slice(b * LANES, (b + 1) * LANES)
         scaled_lines[b * n_rows : (b + 1) * n_rows] = scaled[:, at]
+        block_lines[b * n_rows : (b + 1) * n_rows] = mixed[:n_rows, at]
 
     def finish(first):
-        total = part[...] + matmul(tile[:, first : first + length], other[...])
-        for i in range(n_x):
-            for b in range(n_blocks):
-                out[i, b * per_x : (b + 1) * per_x] = total[
-                    i * per_x : (i + 1) * per_x, b * LANES : (b + 1) * LANES
-                ]
+        for half, (part, other) in enumerate(((part_x, other_x), (part_b, other_b))):
+            total = part[...] + matmul(tile[:, first : first + length], other[...])
+            for i in range(n_x):
+                for b in range(n_blocks):
+                    to = (half * n_blocks + b) * per_x
+                    out[i, to : to + per_x] = total[
+                        i * per_x : (i + 1) * per_x, b * LANES : (b + 1) * LANES
+                    ]
 
     @pl.when(core[0] == 0)
     def _():
@@ -78,7 +82,7 @@
         finish(0)
 
 
-def sum_x_kernel(by_x, own, out, block, lines, total, *, n_rows, n_blocks):
+def sum_x_kernel(by_x, out, total, *, n_rows, n_blocks):
     n_x = by_x.shape[0]
     n_z = out.shape[0]
     running = by_x[0]
@@ -89,14 +93,9 @@
         for b in range(2 * n_blocks):
             first = (b * n_z + z) * n_rows
             out[z, b * n_rows : (b + 1) * n_rows] = total[first : first + n_rows]
-    first = n_blocks * LANES
-    block[...] = own[:n_rows, first:]
-    for b in range(n_blocks):
-        at = slice(first + b * LANES, first + (b + 1) * LANES)
-        lines[b * n_rows : (b + 1) * n_rows] = own[:n_rows, at]
-
-
-def residual_kernel(by_z, scaled, lines, residual, out, mine, *, n_rows, n_blocks):
+
+
+def residual_kernel(by_z, scaled, lines, residual, out, *, n_rows, n_blocks):
     n_lines = n_blocks * n_rows
     running = by_z[0]
     for z in range(1, by_z.shape[0]):
@@ -104,29 +103,30 @@
     rest = running[:n_lines] - scaled[...]
     residual[...] = rest
     squares = rest * rest
-    mine[...] = jnp.zeros(mine.shape, F32)
-    mine[:n_lines] = running[n_lines:]
-    mine[n_lines : 2 * n_lines] = lines[...]
+    out[0, 0] = running[n_lines:]
+    out[0, 1] = lines[...]
+    out[0, 2] = jnp.zeros((n_lines, LANES), F32)
     for b in range(n_blocks):
         at = slice(b * n_rows, (b + 1) * n_rows)
-        mine[2 * n_lines + b : 2 * n_lines + b + 1] = jnp.sum(squares[at], axis=0, keepdims=True)
-    for z in range(out.shape[0]):
-        out[z] = mine[...]
+        out[0, 2, b : b + 1] = jnp.sum(squares[at], axis=0, keepdims=True)
+    for z in range(1, out.shape[0]):
+        out[z] = out[0]
 
 
 def gather_kernel(by_z, out, *, n_rows, n_blocks):
     n_z = by_z.shape[0]
-    n_lines = 2 * n_blocks * n_rows
+    n_lines = n_blocks * n_rows
     for z in range(n_z):
-        for b in range(2 * n_blocks):
-            first = (b * n_z + z) * n_rows
-            out[0, first : first + n_rows] = by_z[z, b * n_rows : (b + 1) * n_rows]
-    running = by_z[0, n_lines : n_lines + n_blocks]
+        for part in range(2):
+            for b in range(n_blocks):
+                first = ((part * n_blocks + b) * n_z + z) * n_rows
+                out[0, first : first + n_rows] = by_z[z, part, b * n_rows : (b + 1) * n_rows]
+    running = by_z[0, 2]
     for z in range(1, n_z):
-        running = running + by_z[z, n_lines : n_lines + n_blocks]
-    last = n_z * n_lines
+        running = running + by_z[z, 2]
+    last = 2 * n_z * n_lines
     out[0, last:] = jnp.zeros((out.shape[1] - last, LANES), F32)
-    out[0, last : last + n_blocks] = running
+    out[0, last : last + n_blocks] = running[:n_blocks]
     for i in range(1, out.shape[0]):
         out[i] = out[0]
 
@@ -150,7 +150,11 @@
     return running
 
 
-def own_kernel(lines, ritz, metric, product, window, *, n_blocks, per_block):
+def own_kernel(
+    lines, mixed, direction, ritz, metric, block, first_rows, product, window, *, n_blocks, per_block
+):
+    block[...] = mixed[: block.shape[0]]
+    first_rows[...] = direction[: block.shape[0]]
     ritz[...], metric[...] = grams(lines, product, window, n_blocks, per_block)
 
 
@@ -184,50 +188,49 @@
     core = lax.axis_index("col")
     sizes = dict(n_rows=n_rows, n_blocks=n_blocks)
 
+    other_x = swap_cores(current_block)
     direction = matmul(correction_block, mixing_coeffs[width : 2 * width]) + matmul(
         previous_block, mixing_coeffs[2 * width :]
     )
     mixed = matmul(current_block, mixing_coeffs[:width]) + direction
-    own = jnp.concatenate([current_block, mixed], axis=1)
+    other_b = swap_cores(mixed)
     scaled_rows = current_block[:n_rows] * ritz_values[None, :]
 
-    other = swap_cores(own)
     tile = hamiltonian_rows.reshape(n_z, n_x, n_rows, n_c * own_len)
     tile = tile.transpose(1, 0, 2, 3).reshape(n_x * per_block, n_c * own_len)
-    part = matmul(lax.dynamic_slice_in_dim(tile, core * own_len, own_len, 1), own)
+    own_tile = lax.dynamic_slice_in_dim(tile, core * own_len, own_len, 1)
     n_sum = 2 * n_blocks * per_block
-    partial, scaled, next_direction = call(
+    partial, scaled, block_lines = call(
         partial_kernel,
         "partial",
-        (shape(n_x, n_sum, LANES), shape(n_lines, LANES), shape(n_rows, width)),
+        (shape(n_x, n_sum, LANES), shape(n_lines, LANES), shape(n_lines, LANES)),
         core.reshape(1),
         tile,
-        other,
-        part,
+        other_x,
+        other_b,
+        matmul(own_tile, current_block),
+        matmul(own_tile, mixed),
         scaled_rows,
-        direction,
-        in_spaces=[pltpu.SMEM] + [pltpu.VMEM] * 5,
+        mixed,
+        in_spaces=[pltpu.SMEM] + [pltpu.VMEM] * 7,
     )
 
     by_x = exchange(partial, "row_1")
-    slots, next_block, block_lines = call(
+    slots = call(
         functools.partial(sum_x_kernel, **sizes),
         "sum_x",
-        (shape(n_z, 2 * n_lines, LANES), shape(n_rows, width), shape(n_lines, LANES)),
+        shape(n_z, 2 * n_lines, LANES),
         by_x,
-        own,
         scratch=[pltpu.VMEM((n_sum, LANES), F32)],
     )
     by_z = exchange(slots, "row_0")
-    n_mine = padded(2 * n_lines + n_blocks)
     residual, mine = call(
         functools.partial(residual_kernel, **sizes),
         "residual",
-        (shape(n_lines, LANES), shape(n_z, n_mine, LANES)),
+        (shape(n_lines, LANES), shape(n_z, 3, n_lines, LANES)),
         by_z,
         scaled,
         block_lines,
-        scratch=[pltpu.VMEM((n_mine, LANES), F32)],
     )
 
     copies = call(
@@ -239,11 +242,13 @@
     lines = exchange(copies, "row_1")
     other_lines = swap_cores(lines)
     scratch = [pltpu.VMEM((n_x * per_block, width), F32)] * 2
-    ritz_part, metric_part = call(
+    ritz_part, metric_part, next_block, next_direction = call(
         functools.partial(own_kernel, n_blocks=n_blocks, per_block=per_block),
         "own_grams",
-        (shape(width, width), shape(width, width)),
+        (shape(width, width), shape(width, width), shape(n_rows, width), shape(n_rows, width)),
         lines,
+        mixed,
+        direction,
         scratch=scratch,
     )
     ritz_matrix, metric_matrix, next_correction = call(

time: 132 us -> 131 us (level)
  starting transfers between devices: 51.1 us -> 54 us
  blocking collectives: 68.8 us -> 67.4 us
    ppermute x2 -> x3, starting transfers between devices: 51.1 us -> 54 us  [swap_cores(): return lax.ppermute(shard, 'col', [(0, 1), (1, 0)])]
    all_to_all x4, blocking collectives: 68.8 us -> 67.4 us  [exchange(): return lax.all_to_all(blocks, axis, 0, 0, tiled=True)]
    dot_general x4 -> x5, matrix products: 3.7 us -> 3.85 us  [matmul(): jnp.dot(left, right, preferred_element_type=F32, precision=lax.Precision....]
  transfers between devices with their start and end apart: 2 -> 3, of which waited for: 2 -> 1; matrix products, arithmetic and copies ran while one was open for 1% -> 3% of each run, Pallas kernels for 0% -> 1%
where the time goes in v4:
time: 131 us
  blocking collectives  67.4 us (51%)
  starting transfers between devices  54 us (41%)
  matrix products  3.85 us (3%)
  Pallas kernels  3.25 us (2%)
    all_to_all x4, blocking collectives, exchange(): return lax.all_to_all(blocks, axis, 0, 0, tiled=True)  67.4 us
    ppermute x3, starting transfers between devices, swap_cores(): return lax.ppermute(shard, 'col', [(0, 1), (1, 0)])  54 us
    dot_general x5, matrix products, matmul(): jnp.dot(left, right, preferred_element_type=F32, precision=lax.Precision....  3.85 us
    pallas_call x6, Pallas kernels, call(): pl.pallas_call(kernel, in_specs=[pl.BlockSpec(memory_space=space) for spa...  3.25 us
  transfers between devices with their start and end apart: 3, of which 1 were waited for; matrix products, arithmetic and copies ran while one was open for 3% of the time, Pallas kernels for 1%

profile of v4, /device:TPU:65, one launch (start us, length us, event | category | flops | bytes accessed | tf_op | source)
XLA Modules:
  0.0 130.6 jit_solution(13488586442954705596)
XLA Ops:
  0.6 0.0 copy-start
  0.6 0.0 copy-start.2
  0.7 43.5 %collective-permute-start = (f32[256,256]{1,0:T(8,128)}, f32[256,256]{1,0:T(8,128)S(1)}, u32[]{:S(2)}, u32[]{:S(2)}) collective-permute-start(f32[256,256]{1,0:T(8,128)} %param.7), channel_id=1, source_target_pairs={{0,1},{1,0},{2,3},{3,2},{4,5},{5,4},{6,7},{7,6},{8,9},{9,8},{10,11... | collective-permute-start | bytes 786440 | tf_op jit(solution)/shard_map/ppermute | solution.py:28
  44.2 0.0 copy-done
  44.2 1.3 %fusion.1 = f32[256,256]{1,0:T(8,128)S(1)} fusion(f32[256,256]{1,0:T(8,128)S(1)} %copy-done, f32[768,256]{1,0:T(8,128)} %param.11), kind=kOutput, calls=%fused_computation.4 | convolution fusion | flops 201326592 | bytes 786432 | tf_op jit(solution)/shard_map/dot_general | solution.py:32
  45.5 0.0 copy-done.2
  45.5 0.0 copy-start.1
  45.5 1.4 %convolution_add_fusion.direction = f32[256,256]{1,0:T(8,128)S(1)} fusion(f32[256,256]{1,0:T(8,128)S(1)} %fusion.1, f32[256,256]{1,0:T(8,128)} %param.9, f32[768,256]{1,0:T(8,128)S(1)} %copy-done.2), kind=kOutput, calls=%fused_computation | convolution fusion | flops 201392128 | bytes 1048576 | tf_op jit(solution)/shard_map/dot_general | solution.py:32
  46.9 0.0 copy-done.1
  46.9 0.0 copy-start.3
  46.9 0.4 convolution_add_fusion.1.mixed
  47.3 2.0 %collective-permute-start.1 = (f32[256,256]{1,0:T(8,128)S(1)}, f32[256,256]{1,0:T(8,128)S(1)}, u32[]{:S(2)}, u32[]{:S(2)}) collective-permute-start(f32[256,256]{1,0:T(8,128)S(1)} %convolution_add_fusion.1.mixed), channel_id=1, source_target_pairs={{0,1},{1,0},{2,3},{3,2},{4,5},{5,4},{6,7},{7,6},{8,9},{9,8},{10,11... | collective-permute-start | bytes 786440 | tf_op jit(solution)/shard_map/ppermute | solution.py:28
  49.3 0.0 copy-done.3
  49.3 0.4 reshape.22.tile
  49.7 0.0 copy-start.4
  49.7 0.4 fusion.4.part_b
  50.1 0.3 copy-done.4
  50.4 0.4 fusion.6.part_x
  50.8 0.0 collective-permute-done.1.other_b
  50.8 0.0 collective-permute-done.other_x
  50.8 0.6 partial.1
  51.4 19.9 %all_to_all.20.by_x = f32[8,128,128]{2,1,0:T(8,128)S(1)} all-to-all(f32[8,128,128]{2,1,0:T(8,128)S(1)} %get-tuple-element.17), channel_id=1, replica_groups=mesh['chan'=2,'row_0'=16,'row_1'=8,'col'=2] {'row_1'}, dimensions={0} | all-to-all | bytes 1048576 | tf_op jit(solution)/shard_map/all_to_all | solution.py:24
  71.3 0.1 sum_x.1
  71.4 17.9 %all_to_all.21.by_z = f32[16,8,128]{2,1,0:T(8,128)S(1)} all-to-all(f32[16,8,128]{2,1,0:T(8,128)S(1)} %sum_x.1), channel_id=1, replica_groups=mesh['chan'=2,'row_0'=16,'row_1'=8,'col'=2] {'row_0'}, dimensions={0} | all-to-all | bytes 131072 | tf_op jit(solution)/shard_map/all_to_all | solution.py:24
  89.3 14.7 %all_to_all.22.by_z = f32[16,3,4,128]{3,2,1,0:T(4,128)S(1)} all-to-all(f32[16,3,4,128]{3,2,1,0:T(4,128)S(1)} %get-tuple-element.20), channel_id=1, replica_groups=mesh['chan'=2,'row_0'=16,'row_1'=8,'col'=2] {'row_0'}, dimensions={0} | all-to-all | bytes 196608 | tf_op jit(solution)/shard_map/all_to_all | solution.py:24
  104.0 0.1 gather.1
  104.1 15.0 %all_to_all.23.lines.own_lines = f32[8,136,128]{2,1,0:T(8,128)S(1)} all-to-all(f32[8,136,128]{2,1,0:T(8,128)S(1)} %gather.1), channel_id=1, replica_groups=mesh['chan'=2,'row_0'=16,'row_1'=8,'col'=2] {'row_1'}, dimensions={0} | all-to-all | bytes 1114112 | tf_op jit(solution)/shard_map/all_to_all | solution.py:24
  119.0 8.5 %collective-permute-start.2 = (f32[8,136,128]{2,1,0:T(8,128)S(1)}, f32[8,136,128]{2,1,0:T(8,128)S(1)}, u32[]{:S(2)}, u32[]{:S(2)}) collective-permute-start(f32[8,136,128]{2,1,0:T(8,128)S(1)} %all_to_all.23.lines.own_lines), channel_id=1, source_target_pairs={{0,1},{1,0},{2,3},{3,2},{4,5},{5,4},{6,7},{7,6},{8,9},{9,8},{10,11... | collective-permute-start | bytes 1671176 | tf_op jit(solution)/shard_map/ppermute | solution.py:28
  127.6 1.0 own_grams.1
  128.6 0.5 collective-permute-done.2.lines
  129.1 1.4 %final.1 = (f32[256,256]{1,0:T(8,128)}, f32[256,256]{1,0:T(8,128)}, f32[2,256]{1,0:T(2,128)}) custom-call(f32[256,256]{1,0:T(8,128)S(1)} %get-tuple-element.23.ritz_part, f32[256,256]{1,0:T(8,128)S(1)} %get-tuple-element.24.metric_part, f32[8,136,128]{2,1,0:T(8,128)S(1)} %collective-permute-done.2.lines, f32[8,136,128]{2,1,0:T(8,128)S(1)} %all_to_all.23.lines.own_lines, ...), custom_call_target="tpu_custom_call" | custom-call | tf_op jit(solution)/shard_map/final/pallas_call | solution.py:38
  (3 shorter events, 0.1 us)
Async XLA Ops:
  0.6 43.5 %copy-start = (f32[256,256]{1,0:T(8,128)S(1)}, f32[256,256]{1,0:T(8,128)}, u32[]{:S(2)}) copy-start(f32[256,256]{1,0:T(8,128)} %param.8) | copy-start | bytes 786436
  0.6 44.9 %copy-start.2 = (f32[768,256]{1,0:T(8,128)S(1)}, f32[768,256]{1,0:T(8,128)}, u32[]{:S(2)}) copy-start(f32[768,256]{1,0:T(8,128)} %param.11) | copy-start | bytes 2359300
  0.7 50.1 %collective-permute-start = (f32[256,256]{1,0:T(8,128)}, f32[256,256]{1,0:T(8,128)S(1)}, u32[]{:S(2)}, u32[]{:S(2)}) collective-permute-start(f32[256,256]{1,0:T(8,128)} %param.7), channel_id=1, source_target_pairs={{0,1},{1,0},{2,3},{3,2},{4,5},{5,4},{6,7},{7,6},{8,9},{9,8},{10,11... | collective-permute-start | bytes 786440 | tf_op jit(solution)/shard_map/ppermute | solution.py:28
  45.5 1.4 %copy-start.1 = (f32[256,256]{1,0:T(8,128)S(1)}, f32[256,256]{1,0:T(8,128)}, u32[]{:S(2)}) copy-start(f32[256,256]{1,0:T(8,128)} %param.7) | copy-start | bytes 786436
  46.9 2.4 %copy-start.3 = (f32[128,1,2,512]{3,2,1,0:T(2,128)S(1)}, f32[128,1,2,512]{3,2,1,0:T(2,128)}, u32[]{:S(2)}) copy-start(f32[128,1,2,512]{3,2,1,0:T(2,128)} %param.6) | copy-start | bytes 1572868
  47.3 3.5 %collective-permute-start.1 = (f32[256,256]{1,0:T(8,128)S(1)}, f32[256,256]{1,0:T(8,128)S(1)}, u32[]{:S(2)}, u32[]{:S(2)}) collective-permute-start(f32[256,256]{1,0:T(8,128)S(1)} %convolution_add_fusion.1.mixed), channel_id=1, source_target_pairs={{0,1},{1,0},{2,3},{3,2},{4,5},{5,4},{6,7},{7,6},{8,9},{9,8},{10,11... | collective-permute-start | bytes 786440 | tf_op jit(solution)/shard_map/ppermute | solution.py:28
  49.7 0.7 copy-start.4
  119.0 10.1 %collective-permute-start.2 = (f32[8,136,128]{2,1,0:T(8,128)S(1)}, f32[8,136,128]{2,1,0:T(8,128)S(1)}, u32[]{:S(2)}, u32[]{:S(2)}) collective-permute-start(f32[8,136,128]{2,1,0:T(8,128)S(1)} %all_to_all.23.lines.own_lines), channel_id=1, source_target_pairs={{0,1},{1,0},{2,3},{3,2},{4,5},{5,4},{6,7},{7,6},{8,9},{9,8},{10,11... | collective-permute-start | bytes 1671176 | tf_op jit(solution)/shard_map/ppermute | solution.py:28

commit v5 on v4

--- a/solution.py
+++ b/solution.py
@@ -51,27 +51,27 @@
 
 
 def partial_kernel(
-    core, tile, other_x, other_b, part_x, part_b, scaled, mixed, out, scaled_lines, block_lines
+    core, tile, other, part, scaled, own, out, scaled_lines, block_lines
 ):
     n_x = out.shape[0]
     n_rows, width = scaled.shape
-    length = other_x.shape[0]
-    per_x = part_x.shape[0] // n_x
+    length = other.shape[0]
+    per_x = part.shape[0] // n_x
     n_blocks = width // LANES
     for b in range(n_blocks):
         at = slice(b * LANES, (b + 1) * LANES)
         scaled_lines[b * n_rows : (b + 1) * n_rows] = scaled[:, at]
-        block_lines[b * n_rows : (b + 1) * n_rows] = mixed[:n_rows, at]
+        block_lines[b * n_rows : (b + 1) * n_rows] = own[
+            :n_rows, width + b * LANES : width + (b + 1) * LANES
+        ]
 
     def finish(first):
-        for half, (part, other) in enumerate(((part_x, other_x), (part_b, other_b))):
-            total = part[...] + matmul(tile[:, first : first + length], other[...])
-            for i in range(n_x):
-                for b in range(n_blocks):
-                    to = (half * n_blocks + b) * per_x
-                    out[i, to : to + per_x] = total[
-                        i * per_x : (i + 1) * per_x, b * LANES : (b + 1) * LANES
-                    ]
+        total = part[...] + matmul(tile[:, first : first + length], other[...])
+        for i in range(n_x):
+            for b in range(2 * n_blocks):
+                out[i, b * per_x : (b + 1) * per_x] = total[
+                    i * per_x : (i + 1) * per_x, b * LANES : (b + 1) * LANES
+                ]
 
     @pl.when(core[0] == 0)
     def _():
@@ -131,8 +131,10 @@
         out[i] = out[0]
 
 
-def grams(lines, product, window, n_blocks, per_block):
-    for i in range(lines.shape[0]):
+def own_kernel(lines, packed, product, window, *, n_blocks, per_block):
+    n_x = lines.shape[0]
+    width = product.shape[1]
+    for i in range(n_x):
         to = slice(i * per_block, (i + 1) * per_block)
         for b in range(n_blocks):
             at = slice(b * LANES, (b + 1) * LANES)
@@ -140,39 +142,30 @@
             first = (n_blocks + b) * per_block
             window[to, at] = lines[i, first : first + per_block]
     turned = window[...].T
-    return matmul(turned, product[...]), matmul(turned, window[...])
-
-
-def square_of(lines, n_gathered, n_blocks):
-    running = lines[0, n_gathered : n_gathered + n_blocks]
-    for i in range(1, lines.shape[0]):
-        running = running + lines[i, n_gathered : n_gathered + n_blocks]
-    return running
-
-
-def own_kernel(
-    lines, mixed, direction, ritz, metric, block, first_rows, product, window, *, n_blocks, per_block
+    packed[:width, :width] = matmul(turned, product[...])
+    packed[:width, width:] = matmul(turned, window[...])
+    last = 2 * n_blocks * per_block
+    running = lines[0, last:]
+    for i in range(1, n_x):
+        running = running + lines[i, last:]
+    packed[width:] = jnp.zeros((packed.shape[0] - width, 2 * width), F32)
+    for b in range(n_blocks):
+        packed[width : width + 1, b * LANES : (b + 1) * LANES] = running[b : b + 1]
+
+
+def final_kernel(
+    mine, other, residual, own, direction, block, first_rows, correction, ritz, metric, *, total
 ):
-    block[...] = mixed[: block.shape[0]]
-    first_rows[...] = direction[: block.shape[0]]
-    ritz[...], metric[...] = grams(lines, product, window, n_blocks, per_block)
-
-
-def final_kernel(
-    ritz_part, metric_part, lines, own_lines, residual, ritz, metric, correction, product, window,
-    *, n_blocks, per_block, total
-):
-    other_ritz, other_metric = grams(lines, product, window, n_blocks, per_block)
-    ritz[...] = ritz_part[...] + other_ritz
-    metric[...] = metric_part[...] + other_metric
-    n_rows = correction.shape[0]
-    n_gathered = 2 * n_blocks * per_block
-    squares = square_of(own_lines, n_gathered, n_blocks) + square_of(lines, n_gathered, n_blocks)
+    n_rows, width = block.shape
+    block[...] = own[:n_rows, width:]
+    first_rows[...] = direction[:n_rows]
+    ritz[...] = mine[:width, :width] + other[:width, :width]
+    metric[...] = mine[:width, width:] + other[:width, width:]
+    squares = mine[width : width + 1, :width] + other[width : width + 1, :width]
     scale = lax.rsqrt(squares / total + 1e-06)
-    for b in range(n_blocks):
-        correction[:, b * LANES : (b + 1) * LANES] = (
-            residual[b * n_rows : (b + 1) * n_rows] * scale[b : b + 1]
-        )
+    for b in range(width // LANES):
+        at = slice(b * LANES, (b + 1) * LANES)
+        correction[:, at] = residual[b * n_rows : (b + 1) * n_rows] * scale[:, at]
 
 
 def on_device(
@@ -188,12 +181,12 @@
     core = lax.axis_index("col")
     sizes = dict(n_rows=n_rows, n_blocks=n_blocks)
 
-    other_x = swap_cores(current_block)
     direction = matmul(correction_block, mixing_coeffs[width : 2 * width]) + matmul(
         previous_block, mixing_coeffs[2 * width :]
     )
     mixed = matmul(current_block, mixing_coeffs[:width]) + direction
-    other_b = swap_cores(mixed)
+    own = jnp.concatenate([current_block, mixed], axis=1)
+    other = swap_cores(own)
     scaled_rows = current_block[:n_rows] * ritz_values[None, :]
 
     tile = hamiltonian_rows.reshape(n_z, n_x, n_rows, n_c * own_len)
@@ -206,13 +199,11 @@
         (shape(n_x, n_sum, LANES), shape(n_lines, LANES), shape(n_lines, LANES)),
         core.reshape(1),
         tile,
-        other_x,
-        other_b,
-        matmul(own_tile, current_block),
-        matmul(own_tile, mixed),
+        other,
+        matmul(own_tile, own),
         scaled_rows,
-        mixed,
-        in_spaces=[pltpu.SMEM] + [pltpu.VMEM] * 7,
+        own,
+        in_spaces=[pltpu.SMEM] + [pltpu.VMEM] * 5,
     )
 
     by_x = exchange(partial, "row_1")
@@ -240,31 +231,23 @@
         exchange(mine, "row_0"),
     )
     lines = exchange(copies, "row_1")
-    other_lines = swap_cores(lines)
-    scratch = [pltpu.VMEM((n_x * per_block, width), F32)] * 2
-    ritz_part, metric_part, next_block, next_direction = call(
+    packed = call(
         functools.partial(own_kernel, n_blocks=n_blocks, per_block=per_block),
         "own_grams",
-        (shape(width, width), shape(width, width), shape(n_rows, width), shape(n_rows, width)),
+        shape(width + SUBLANES, 2 * width),
         lines,
-        mixed,
+        scratch=[pltpu.VMEM((n_x * per_block, width), F32)] * 2,
+    )
+    return call(
+        functools.partial(final_kernel, total=window_total),
+        "final",
+        (shape(n_rows, width),) * 3 + (shape(width, width),) * 2,
+        packed,
+        swap_cores(packed),
+        residual,
+        own,
         direction,
-        scratch=scratch,
-    )
-    ritz_matrix, metric_matrix, next_correction = call(
-        functools.partial(
-            final_kernel, n_blocks=n_blocks, per_block=per_block, total=window_total
-        ),
-        "final",
-        (shape(width, width), shape(width, width), shape(n_rows, width)),
-        ritz_part,
-        metric_part,
-        other_lines,
-        lines,
-        residual,
-        scratch=scratch,
-    )
-    return (next_block, next_direction, next_correction, ritz_matrix, metric_matrix)
+    )
 
 
 def solution(mesh):

time: 131 us -> 130 us (level)
  starting transfers between devices: 54 us -> 51.1 us
  waiting for transfers between devices: 0.53 us -> 1.94 us
    ppermute x3 -> x2, starting transfers between devices: 54 us -> 51.1 us  [swap_cores(): return lax.ppermute(shard, 'col', [(0, 1), (1, 0)])]
    ppermute x3 -> x2, waiting for transfers between devices: 0.53 us -> 1.94 us  [swap_cores(): return lax.ppermute(shard, 'col', [(0, 1), (1, 0)])]
    dot_general x5 -> x4, matrix products: 3.85 us -> 3.7 us  [matmul(): jnp.dot(left, right, preferred_element_type=F32, precision=lax.Precision....]
  transfers between devices with their start and end apart: 3 -> 2, of which waited for: 1 -> 2; matrix products, arithmetic and copies ran while one was open for 3% -> 1% of each run, Pallas kernels for 1% -> 0%
where the time goes in v5:
time: 130 us
  blocking collectives  68.7 us (53%)
  starting transfers between devices  51.1 us (39%)
  matrix products  3.7 us (3%)
  Pallas kernels  2.26 us (2%)
  waiting for transfers between devices  1.94 us (1%)
  local copies, waits for them, and re-layouts  1.4 us (1%)
    all_to_all x4, blocking collectives, exchange(): return lax.all_to_all(blocks, axis, 0, 0, tiled=True)  68.7 us
    ppermute x2, starting transfers between devices, swap_cores(): return lax.ppermute(shard, 'col', [(0, 1), (1, 0)])  51.1 us
    dot_general x4, matrix products, matmul(): jnp.dot(left, right, preferred_element_type=F32, precision=lax.Precision....  3.7 us
  transfers between devices with their start and end apart: 2, of which 2 were waited for; matrix products, arithmetic and copies ran while one was open for 1% of the time, Pallas kernels for 0%

profile of v5, /device:TPU:65, one launch (start us, length us, event | category | flops | bytes accessed | tf_op | source)
XLA Modules:
  0.0 130.0 jit_solution(10754941026643753992)
XLA Ops:
  0.6 0.0 copy-start
  0.6 0.0 copy-start.2
  0.7 0.9 copy-done
  1.6 1.3 %fusion.3 = f32[256,256]{1,0:T(8,128)S(1)} fusion(f32[256,256]{1,0:T(8,128)S(1)} %copy-done, f32[768,256]{1,0:T(8,128)} %param.11), kind=kOutput, calls=%fused_computation.7 | convolution fusion | flops 201326592 | bytes 786432 | tf_op jit(solution)/shard_map/dot_general | solution.py:32
  2.9 0.0 copy-done.2
  2.9 0.0 copy-start.1
  2.9 1.4 %convolution_add_fusion.direction = f32[256,256]{1,0:T(8,128)S(1)} fusion(f32[256,256]{1,0:T(8,128)S(1)} %fusion.3, f32[256,256]{1,0:T(8,128)} %param.9, f32[768,256]{1,0:T(8,128)S(1)} %copy-done.2), kind=kOutput, calls=%fused_computation | convolution fusion | flops 201392128 | bytes 1048576 | tf_op jit(solution)/shard_map/dot_general | solution.py:32
  4.3 0.0 copy-done.1
  4.3 0.4 convolution_add_fusion.1
  4.7 0.0 copy-start.3
  4.7 0.1 pad_maximum_fusion.own
  4.8 43.5 %collective-permute-start = (f32[256,512]{1,0:T(8,128)S(1)}, f32[256,512]{1,0:T(8,128)S(1)}, u32[]{:S(2)}, u32[]{:S(2)}) collective-permute-start(f32[256,512]{1,0:T(8,128)S(1)} %pad_maximum_fusion.own), channel_id=1, source_target_pairs={{0,1},{1,0},{2,3},{3,2},{4,5},{5,4},{6,7},{7,6},{8,9},{9,8},{10,11... | collective-permute-start | bytes 1572872 | tf_op jit(solution)/shard_map/ppermute | solution.py:28
  48.3 0.0 copy-done.3
  48.4 0.4 reshape.22.tile
  48.7 0.0 copy-start.4
  48.8 0.6 fusion.part
  49.4 0.0 copy-done.4
  49.4 0.4 collective-permute-done.other
  49.8 0.6 partial.1
  50.5 20.4 %all_to_all.20.by_x = f32[8,128,128]{2,1,0:T(8,128)S(1)} all-to-all(f32[8,128,128]{2,1,0:T(8,128)S(1)} %get-tuple-element.10), channel_id=1, replica_groups=mesh['chan'=2,'row_0'=16,'row_1'=8,'col'=2] {'row_1'}, dimensions={0} | all-to-all | bytes 1048576 | tf_op jit(solution)/shard_map/all_to_all | solution.py:24
  70.9 0.1 sum_x.1
  70.9 17.7 %all_to_all.21.by_z = f32[16,8,128]{2,1,0:T(8,128)S(1)} all-to-all(f32[16,8,128]{2,1,0:T(8,128)S(1)} %sum_x.1), channel_id=1, replica_groups=mesh['chan'=2,'row_0'=16,'row_1'=8,'col'=2] {'row_0'}, dimensions={0} | all-to-all | bytes 131072 | tf_op jit(solution)/shard_map/all_to_all | solution.py:24
  88.6 14.7 %all_to_all.22.by_z = f32[16,3,4,128]{3,2,1,0:T(4,128)S(1)} all-to-all(f32[16,3,4,128]{3,2,1,0:T(4,128)S(1)} %get-tuple-element.13), channel_id=1, replica_groups=mesh['chan'=2,'row_0'=16,'row_1'=8,'col'=2] {'row_0'}, dimensions={0} | all-to-all | bytes 196608 | tf_op jit(solution)/shard_map/all_to_all | solution.py:24
  103.3 0.1 gather.1
  103.4 15.9 %all_to_all.23.lines = f32[8,136,128]{2,1,0:T(8,128)S(1)} all-to-all(f32[8,136,128]{2,1,0:T(8,128)S(1)} %gather.1), channel_id=1, replica_groups=mesh['chan'=2,'row_0'=16,'row_1'=8,'col'=2] {'row_1'}, dimensions={0} | all-to-all | bytes 1114112 | tf_op jit(solution)/shard_map/all_to_all | solution.py:24
  119.3 0.6 own_grams.1.mine
  120.0 7.6 %collective-permute-start.1 = (f32[264,512]{1,0:T(8,128)S(1)}, f32[264,512]{1,0:T(8,128)S(1)}, u32[]{:S(2)}, u32[]{:S(2)}) collective-permute-start(f32[264,512]{1,0:T(8,128)S(1)} %own_grams.1.mine), channel_id=1, source_target_pairs={{0,1},{1,0},{2,3},{3,2},{4,5},{5,4},{6,7},{7,6},{8,9},{9,8},{10,11... | collective-permute-start | bytes 1622024 | tf_op jit(solution)/shard_map/ppermute | solution.py:28
  127.6 1.5 %collective-permute-done.1.other = f32[264,512]{1,0:T(8,128)S(1)} collective-permute-done((f32[264,512]{1,0:T(8,128)S(1)}, f32[264,512]{1,0:T(8,128)S(1)}, u32[]{:S(2)}, u32[]{:S(2)}) %collective-permute-start.1) | collective-permute-done | bytes 540704 | tf_op jit(solution)/shard_map/ppermute | solution.py:28
  129.1 0.9 final.1
  (3 shorter events, 0.1 us)
Async XLA Ops:
  0.6 1.0 copy-start
  0.6 2.3 %copy-start.2 = (f32[768,256]{1,0:T(8,128)S(1)}, f32[768,256]{1,0:T(8,128)}, u32[]{:S(2)}) copy-start(f32[768,256]{1,0:T(8,128)} %param.11) | copy-start | bytes 2359300
  2.9 1.4 %copy-start.1 = (f32[256,256]{1,0:T(8,128)S(1)}, f32[256,256]{1,0:T(8,128)}, u32[]{:S(2)}) copy-start(f32[256,256]{1,0:T(8,128)} %param.7) | copy-start | bytes 786436
  4.7 43.6 %copy-start.3 = (f32[128,1,2,512]{3,2,1,0:T(2,128)S(1)}, f32[128,1,2,512]{3,2,1,0:T(2,128)}, u32[]{:S(2)}) copy-start(f32[128,1,2,512]{3,2,1,0:T(2,128)} %param.6) | copy-start | bytes 1572868
  4.8 45.0 %collective-permute-start = (f32[256,512]{1,0:T(8,128)S(1)}, f32[256,512]{1,0:T(8,128)S(1)}, u32[]{:S(2)}, u32[]{:S(2)}) collective-permute-start(f32[256,512]{1,0:T(8,128)S(1)} %pad_maximum_fusion.own), channel_id=1, source_target_pairs={{0,1},{1,0},{2,3},{3,2},{4,5},{5,4},{6,7},{7,6},{8,9},{9,8},{10,11... | collective-permute-start | bytes 1572872 | tf_op jit(solution)/shard_map/ppermute | solution.py:28
  48.7 0.7 copy-start.4
  120.0 9.1 %collective-permute-start.1 = (f32[264,512]{1,0:T(8,128)S(1)}, f32[264,512]{1,0:T(8,128)S(1)}, u32[]{:S(2)}, u32[]{:S(2)}) collective-permute-start(f32[264,512]{1,0:T(8,128)S(1)} %own_grams.1.mine), channel_id=1, source_target_pairs={{0,1},{1,0},{2,3},{3,2},{4,5},{5,4},{6,7},{7,6},{8,9},{9,8},{10,11... | collective-permute-start | bytes 1622024 | tf_op jit(solution)/shard_map/ppermute | solution.py:28

commit v6 on v5

--- a/solution.py
+++ b/solution.py
@@ -48,6 +48,14 @@
 
 def padded(count):
     return -(-count // SUBLANES) * SUBLANES
+
+
+def mix_kernel(x, w, p, c, own, direction):
+    width = x.shape[1]
+    total = matmul(w[...], c[width : 2 * width]) + matmul(p[...], c[2 * width :])
+    direction[...] = total[: direction.shape[0]]
+    own[:, :width] = x[...]
+    own[:, width:] = total + matmul(x[...], c[:width])
 
 
 def partial_kernel(
@@ -181,16 +189,22 @@
     core = lax.axis_index("col")
     sizes = dict(n_rows=n_rows, n_blocks=n_blocks)
 
-    direction = matmul(correction_block, mixing_coeffs[width : 2 * width]) + matmul(
-        previous_block, mixing_coeffs[2 * width :]
-    )
-    mixed = matmul(current_block, mixing_coeffs[:width]) + direction
-    own = jnp.concatenate([current_block, mixed], axis=1)
+    tile = hamiltonian_rows.reshape(n_z, n_x, n_rows, n_c * own_len)
+    tile = tile.transpose(1, 0, 2, 3).reshape(n_x * per_block, n_c * own_len)
+    tile, correction_block = lax.optimization_barrier((tile, correction_block))
+
+    own, direction = call(
+        mix_kernel,
+        "mix",
+        (shape(own_len, 2 * width), shape(n_rows, width)),
+        current_block,
+        correction_block,
+        previous_block,
+        mixing_coeffs,
+    )
     other = swap_cores(own)
     scaled_rows = current_block[:n_rows] * ritz_values[None, :]
 
-    tile = hamiltonian_rows.reshape(n_z, n_x, n_rows, n_c * own_len)
-    tile = tile.transpose(1, 0, 2, 3).reshape(n_x * per_block, n_c * own_len)
     own_tile = lax.dynamic_slice_in_dim(tile, core * own_len, own_len, 1)
     n_sum = 2 * n_blocks * per_block
     partial, scaled, block_lines = call(

time: 130 us -> 129 us (level)
  matrix products: 3.7 us -> 0.61 us
  local copies, waits for them, and re-layouts: 1.4 us -> 2.92 us
    dot_general x4 -> x1, matrix products: 3.7 us -> 0.61 us  [matmul(): jnp.dot(left, right, preferred_element_type=F32, precision=lax.Precision....]
    pallas_call x6 -> x7, Pallas kernels: 2.26 us -> 3.11 us  [call(): pl.pallas_call(kernel, in_specs=[pl.BlockSpec(memory_space=space) for spa...]
  transfers between devices with their start and end apart: 2 -> 2, of which waited for: 2 -> 2; matrix products, arithmetic and copies ran while one was open for 1% -> 0% of each run, Pallas kernels for 0% -> 0%
where the time goes in v6:
time: 129 us
  blocking collectives  68.7 us (53%)
  starting transfers between devices  51 us (40%)
  Pallas kernels  3.11 us (2%)
  local copies, waits for them, and re-layouts  2.92 us (2%)
  waiting for transfers between devices  1.74 us (1%)
    all_to_all x4, blocking collectives, exchange(): return lax.all_to_all(blocks, axis, 0, 0, tiled=True)  68.7 us
    ppermute x2, starting transfers between devices, swap_cores(): return lax.ppermute(shard, 'col', [(0, 1), (1, 0)])  51 us
    pallas_call x7, Pallas kernels, call(): pl.pallas_call(kernel, in_specs=[pl.BlockSpec(memory_space=space) for spa...  3.11 us
  transfers between devices with their start and end apart: 2, of which 2 were waited for; matrix products, arithmetic and copies ran while one was open for 0% of the time, Pallas kernels for 0%

profile of v6, /device:TPU:65, one launch (start us, length us, event | category | flops | bytes accessed | tf_op | source)
XLA Modules:
  0.0 128.8 jit_solution(8374845910109601361)
XLA Ops:
  0.6 0.0 copy-start
  0.6 1.1 copy_bitcast_fusion
  1.8 0.0 copy-start.1
  1.8 0.0 copy-start.2
  1.8 0.0 copy-start.3
  1.8 0.4 reshape.22.tile
  2.2 0.0 copy-done
  2.2 0.6 copy-done.1
  2.8 0.1 copy-done.2
  2.9 0.1 copy-done.3
  2.9 0.9 mix.1
  3.8 43.4 %collective-permute-start = (f32[256,512]{1,0:T(8,128)S(1)}, f32[256,512]{1,0:T(8,128)S(1)}, u32[]{:S(2)}, u32[]{:S(2)}) collective-permute-start(f32[256,512]{1,0:T(8,128)S(1)} %get-tuple-element.16.own), channel_id=1, source_target_pairs={{0,1},{1,0},{2,3},{3,2},{4,5},{5,4},{6,7},{7,6},{8,9},{9,8},{10,11... | collective-permute-start | bytes 1572872 | tf_op jit(solution)/shard_map/ppermute | solution.py:28
  47.2 0.0 copy-start.4
  47.2 0.7 copy-done.4
  47.9 0.6 fusion.part
  48.5 0.2 collective-permute-done.other
  48.7 0.6 partial.1
  49.3 20.4 %all_to_all.20.by_x = f32[8,128,128]{2,1,0:T(8,128)S(1)} all-to-all(f32[8,128,128]{2,1,0:T(8,128)S(1)} %get-tuple-element.17), channel_id=1, replica_groups=mesh['chan'=2,'row_0'=16,'row_1'=8,'col'=2] {'row_1'}, dimensions={0} | all-to-all | bytes 1048576 | tf_op jit(solution)/shard_map/all_to_all | solution.py:24
  69.7 0.1 sum_x.1
  69.8 17.7 %all_to_all.21.by_z = f32[16,8,128]{2,1,0:T(8,128)S(1)} all-to-all(f32[16,8,128]{2,1,0:T(8,128)S(1)} %sum_x.1), channel_id=1, replica_groups=mesh['chan'=2,'row_0'=16,'row_1'=8,'col'=2] {'row_0'}, dimensions={0} | all-to-all | bytes 131072 | tf_op jit(solution)/shard_map/all_to_all | solution.py:24
  87.5 14.7 %all_to_all.22.by_z = f32[16,3,4,128]{3,2,1,0:T(4,128)S(1)} all-to-all(f32[16,3,4,128]{3,2,1,0:T(4,128)S(1)} %get-tuple-element.20), channel_id=1, replica_groups=mesh['chan'=2,'row_0'=16,'row_1'=8,'col'=2] {'row_0'}, dimensions={0} | all-to-all | bytes 196608 | tf_op jit(solution)/shard_map/all_to_all | solution.py:24
  102.2 0.1 gather.1
  102.3 15.9 %all_to_all.23.lines = f32[8,136,128]{2,1,0:T(8,128)S(1)} all-to-all(f32[8,136,128]{2,1,0:T(8,128)S(1)} %gather.1), channel_id=1, replica_groups=mesh['chan'=2,'row_0'=16,'row_1'=8,'col'=2] {'row_1'}, dimensions={0} | all-to-all | bytes 1114112 | tf_op jit(solution)/shard_map/all_to_all | solution.py:24
  118.2 0.6 own_grams.1.mine
  118.8 7.6 %collective-permute-start.1 = (f32[264,512]{1,0:T(8,128)S(1)}, f32[264,512]{1,0:T(8,128)S(1)}, u32[]{:S(2)}, u32[]{:S(2)}) collective-permute-start(f32[264,512]{1,0:T(8,128)S(1)} %own_grams.1.mine), channel_id=1, source_target_pairs={{0,1},{1,0},{2,3},{3,2},{4,5},{5,4},{6,7},{7,6},{8,9},{9,8},{10,11... | collective-permute-start | bytes 1622024 | tf_op jit(solution)/shard_map/ppermute | solution.py:28
  126.4 1.5 %collective-permute-done.1.other = f32[264,512]{1,0:T(8,128)S(1)} collective-permute-done((f32[264,512]{1,0:T(8,128)S(1)}, f32[264,512]{1,0:T(8,128)S(1)}, u32[]{:S(2)}, u32[]{:S(2)}) %collective-permute-start.1) | collective-permute-done | bytes 540704 | tf_op jit(solution)/shard_map/ppermute | solution.py:28
  127.9 0.9 final.1
  (2 shorter events, 0.0 us)
Async XLA Ops:
  0.6 1.6 %copy-start = (f32[768,256]{1,0:T(8,128)S(1)}, f32[768,256]{1,0:T(8,128)}, u32[]{:S(2)}) copy-start(f32[768,256]{1,0:T(8,128)} %c.1) | copy-start | bytes 2359300
  1.8 1.0 copy-start.1
  1.8 1.0 copy-start.2
  1.8 1.1 copy-start.3
  3.8 44.9 %collective-permute-start = (f32[256,512]{1,0:T(8,128)S(1)}, f32[256,512]{1,0:T(8,128)S(1)}, u32[]{:S(2)}, u32[]{:S(2)}) collective-permute-start(f32[256,512]{1,0:T(8,128)S(1)} %get-tuple-element.16.own), channel_id=1, source_target_pairs={{0,1},{1,0},{2,3},{3,2},{4,5},{5,4},{6,7},{7,6},{8,9},{9,8},{10,11... | collective-permute-start | bytes 1572872 | tf_op jit(solution)/shard_map/ppermute | solution.py:28
  47.2 0.7 copy-start.4
  118.8 9.1 %collective-permute-start.1 = (f32[264,512]{1,0:T(8,128)S(1)}, f32[264,512]{1,0:T(8,128)S(1)}, u32[]{:S(2)}, u32[]{:S(2)}) collective-permute-start(f32[264,512]{1,0:T(8,128)S(1)} %own_grams.1.mine), channel_id=1, source_target_pairs={{0,1},{1,0},{2,3},{3,2},{4,5},{5,4},{6,7},{7,6},{8,9},{9,8},{10,11... | collective-permute-start | bytes 1622024 | tf_op jit(solution)/shard_map/ppermute | solution.py:28

commit v7 on v6

--- a/solution.py
+++ b/solution.py
@@ -44,6 +44,10 @@
         compiler_params=pltpu.CompilerParams(vmem_limit_bytes=VMEM_BYTES),
         name=name,
     )(*args)
+
+
+def both_cores(shard):
+    return lax.all_gather(shard, "col")
 
 
 def padded(count):
@@ -150,30 +154,47 @@
             first = (n_blocks + b) * per_block
             window[to, at] = lines[i, first : first + per_block]
     turned = window[...].T
-    packed[:width, :width] = matmul(turned, product[...])
-    packed[:width, width:] = matmul(turned, window[...])
+    ritz = matmul(turned, product[...])
+    metric = matmul(turned, window[...])
+    at = n_blocks * width
+    for b in range(n_blocks):
+        lanes = slice(b * LANES, (b + 1) * LANES)
+        packed[b * width : (b + 1) * width] = ritz[:, lanes]
+        packed[at : at + (b + 1) * LANES] = metric[: (b + 1) * LANES, lanes]
+        at += (b + 1) * LANES
     last = 2 * n_blocks * per_block
     running = lines[0, last:]
     for i in range(1, n_x):
         running = running + lines[i, last:]
-    packed[width:] = jnp.zeros((packed.shape[0] - width, 2 * width), F32)
-    for b in range(n_blocks):
-        packed[width : width + 1, b * LANES : (b + 1) * LANES] = running[b : b + 1]
+    packed[at:] = running
 
 
 def final_kernel(
-    mine, other, residual, own, direction, block, first_rows, correction, ritz, metric, *, total
+    packed, residual, own, direction, block, first_rows, correction, ritz, metric, *, total
 ):
     n_rows, width = block.shape
+    n_blocks = width // LANES
     block[...] = own[:n_rows, width:]
     first_rows[...] = direction[:n_rows]
-    ritz[...] = mine[:width, :width] + other[:width, :width]
-    metric[...] = mine[:width, width:] + other[:width, width:]
-    squares = mine[width : width + 1, :width] + other[width : width + 1, :width]
-    scale = lax.rsqrt(squares / total + 1e-06)
-    for b in range(width // LANES):
-        at = slice(b * LANES, (b + 1) * LANES)
-        correction[:, at] = residual[b * n_rows : (b + 1) * n_rows] * scale[:, at]
+
+    def both(first, count):
+        return packed[0, first : first + count] + packed[1, first : first + count]
+
+    at = n_blocks * width
+    for b in range(n_blocks):
+        lanes = slice(b * LANES, (b + 1) * LANES)
+        ritz[:, lanes] = both(b * width, width)
+        for r in range(b + 1):
+            rows = slice(r * LANES, (r + 1) * LANES)
+            piece = both(at + r * LANES, LANES)
+            metric[rows, lanes] = piece
+            if r != b:
+                metric[lanes, rows] = piece.T
+        at += (b + 1) * LANES
+    scale = lax.rsqrt(both(at, n_blocks) / total + 1e-06)
+    for b in range(n_blocks):
+        lanes = slice(b * LANES, (b + 1) * LANES)
+        correction[:, lanes] = residual[b * n_rows : (b + 1) * n_rows] * scale[b : b + 1]
 
 
 def on_device(
@@ -245,10 +266,11 @@
         exchange(mine, "row_0"),
     )
     lines = exchange(copies, "row_1")
+    packed_lines = n_blocks * width + n_blocks * (n_blocks + 1) // 2 * LANES + padded(n_blocks)
     packed = call(
         functools.partial(own_kernel, n_blocks=n_blocks, per_block=per_block),
         "own_grams",
-        shape(width + SUBLANES, 2 * width),
+        shape(packed_lines, LANES),
         lines,
         scratch=[pltpu.VMEM((n_x * per_block, width), F32)] * 2,
     )
@@ -256,8 +278,7 @@
         functools.partial(final_kernel, total=window_total),
         "final",
         (shape(n_rows, width),) * 3 + (shape(width, width),) * 2,
-        packed,
-        swap_cores(packed),
+        both_cores(packed),
         residual,
         own,
         direction,

time: 129 us -> 128 us (level)
  blocking collectives: 68.7 us -> 76.5 us
  starting transfers between devices: 51 us -> 43.4 us
  waiting for transfers between devices: 1.74 us -> 0.2 us
    all_gather x0 -> x1, blocking collectives: none -> 7.8 us  [both_cores(): return lax.all_gather(shard, 'col')]
    ppermute x2 -> x1, starting transfers between devices: 51 us -> 43.4 us  [swap_cores(): return lax.ppermute(shard, 'col', [(0, 1), (1, 0)])]
    ppermute x2 -> x1, waiting for transfers between devices: 1.74 us -> 0.2 us  [swap_cores(): return lax.ppermute(shard, 'col', [(0, 1), (1, 0)])]
  transfers between devices with their start and end apart: 2 -> 1, of which waited for: 2 -> 1; matrix products, arithmetic and copies ran while one was open for 0% -> 0% of each run, Pallas kernels for 0% -> 0%
where the time goes in v7:
time: 128 us; the launch traced here: 127 us
  blocking collectives  76.5 us (60%)
  starting transfers between devices  43.4 us (34%)
  Pallas kernels  3.09 us (2%)
  local copies, waits for them, and re-layouts  2.92 us (2%)
    all_to_all x4, blocking collectives, exchange(): return lax.all_to_all(blocks, axis, 0, 0, tiled=True)  68.7 us
    ppermute x1, starting transfers between devices, swap_cores(): return lax.ppermute(shard, 'col', [(0, 1), (1, 0)])  43.4 us
    all_gather x1, blocking collectives, both_cores(): return lax.all_gather(shard, 'col')  7.8 us
    pallas_call x7, Pallas kernels, call(): pl.pallas_call(kernel, in_specs=[pl.BlockSpec(memory_space=space) for spa...  3.09 us
  transfers between devices with their start and end apart: 1, of which 1 were waited for; matrix products, arithmetic and copies ran while one was open for 0% of the time, Pallas kernels for 0%

profile of v7, /device:TPU:65, one launch (start us, length us, event | category | flops | bytes accessed | tf_op | source)
XLA Modules:
  0.0 127.4 jit_solution(4642670031081225645)
XLA Ops:
  0.6 0.0 copy-start
  0.6 1.1 copy_bitcast_fusion
  1.8 0.0 copy-start.1
  1.8 0.0 copy-start.2
  1.8 0.0 copy-start.3
  1.8 0.4 reshape.22.tile
  2.2 0.0 copy-done
  2.2 0.6 copy-done.1
  2.8 0.1 copy-done.2
  2.9 0.1 copy-done.3
  2.9 0.9 mix.1
  3.8 43.4 %collective-permute-start = (f32[256,512]{1,0:T(8,128)S(1)}, f32[256,512]{1,0:T(8,128)S(1)}, u32[]{:S(2)}, u32[]{:S(2)}) collective-permute-start(f32[256,512]{1,0:T(8,128)S(1)} %get-tuple-element.16.own), channel_id=1, source_target_pairs={{0,1},{1,0},{2,3},{3,2},{4,5},{5,4},{6,7},{7,6},{8,9},{9,8},{10,11... | collective-permute-start | bytes 1572872 | tf_op jit(solution)/shard_map/ppermute | solution.py:28
  47.2 0.0 copy-start.4
  47.2 0.7 copy-done.4
  47.9 0.6 fusion.part
  48.5 0.2 collective-permute-done.other
  48.7 0.6 partial.1
  49.3 20.4 %all_to_all.20.by_x = f32[8,128,128]{2,1,0:T(8,128)S(1)} all-to-all(f32[8,128,128]{2,1,0:T(8,128)S(1)} %get-tuple-element.17), channel_id=1, replica_groups=mesh['chan'=2,'row_0'=16,'row_1'=8,'col'=2] {'row_1'}, dimensions={0} | all-to-all | bytes 1048576 | tf_op jit(solution)/shard_map/all_to_all | solution.py:24
  69.7 0.1 sum_x.1
  69.8 17.7 %all_to_all.21.by_z = f32[16,8,128]{2,1,0:T(8,128)S(1)} all-to-all(f32[16,8,128]{2,1,0:T(8,128)S(1)} %sum_x.1), channel_id=1, replica_groups=mesh['chan'=2,'row_0'=16,'row_1'=8,'col'=2] {'row_0'}, dimensions={0} | all-to-all | bytes 131072 | tf_op jit(solution)/shard_map/all_to_all | solution.py:24
  87.5 14.7 %all_to_all.22.by_z = f32[16,3,4,128]{3,2,1,0:T(4,128)S(1)} all-to-all(f32[16,3,4,128]{3,2,1,0:T(4,128)S(1)} %get-tuple-element.20), channel_id=1, replica_groups=mesh['chan'=2,'row_0'=16,'row_1'=8,'col'=2] {'row_0'}, dimensions={0} | all-to-all | bytes 196608 | tf_op jit(solution)/shard_map/all_to_all | solution.py:24
  102.2 0.1 gather.1
  102.3 15.9 %all_to_all.23.lines = f32[8,136,128]{2,1,0:T(8,128)S(1)} all-to-all(f32[8,136,128]{2,1,0:T(8,128)S(1)} %gather.1), channel_id=1, replica_groups=mesh['chan'=2,'row_0'=16,'row_1'=8,'col'=2] {'row_1'}, dimensions={0} | all-to-all | bytes 1114112 | tf_op jit(solution)/shard_map/all_to_all | solution.py:24
  118.2 0.6 own_grams.1
  118.8 7.8 %all-gather = f32[1808,128]{1,0:T(8,128)S(1)} all-gather(f32[904,128]{1,0:T(8,128)S(1)} %own_grams.1), channel_id=2, replica_groups=mesh['chan'=2,'row_0'=16,'row_1'=8,'col'=2] {'col'}, dimensions={0}, use_global_device_ids=true | all-gather | bytes 1388544 | tf_op jit(solution)/shard_map/all_gather | solution.py:50
  126.6 0.8 final.1
  (2 shorter events, 0.0 us)
Async XLA Ops:
  0.6 1.6 %copy-start = (f32[768,256]{1,0:T(8,128)S(1)}, f32[768,256]{1,0:T(8,128)}, u32[]{:S(2)}) copy-start(f32[768,256]{1,0:T(8,128)} %c.1) | copy-start | bytes 2359300
  1.8 1.0 copy-start.1
  1.8 1.0 copy-start.2
  1.8 1.1 copy-start.3
  3.8 44.9 %collective-permute-start = (f32[256,512]{1,0:T(8,128)S(1)}, f32[256,512]{1,0:T(8,128)S(1)}, u32[]{:S(2)}, u32[]{:S(2)}) collective-permute-start(f32[256,512]{1,0:T(8,128)S(1)} %get-tuple-element.16.own), channel_id=1, source_target_pairs={{0,1},{1,0},{2,3},{3,2},{4,5},{5,4},{6,7},{7,6},{8,9},{9,8},{10,11... | collective-permute-start | bytes 1572872 | tf_op jit(solution)/shard_map/ppermute | solution.py:28
  47.2 0.7 copy-start.4

commit v8 on v7

--- a/solution.py
+++ b/solution.py
@@ -32,7 +32,7 @@
     return jnp.dot(left, right, preferred_element_type=F32, precision=lax.Precision.HIGHEST)
 
 
-def call(kernel, name, out_shape, *args, in_spaces=None, scratch=()):
+def call(kernel, name, out_shape, *args, in_spaces=None, scratch=(), cost=None):
     spaces = in_spaces or [pltpu.VMEM] * len(args)
     resident = pl.BlockSpec(memory_space=pltpu.VMEM)
     return pl.pallas_call(
@@ -42,6 +42,7 @@
         out_shape=out_shape,
         scratch_shapes=scratch,
         compiler_params=pltpu.CompilerParams(vmem_limit_bytes=VMEM_BYTES),
+        cost_estimate=cost,
         name=name,
     )(*args)
 
@@ -54,7 +55,11 @@
     return -(-count // SUBLANES) * SUBLANES
 
 
-def mix_kernel(x, w, p, c, own, direction):
+def order_kernel(core, out):
+    out[...] = jnp.full(out.shape, core[0].astype(F32))
+
+
+def mix_kernel(order, x, w, p, c, own, direction):
     width = x.shape[1]
     total = matmul(w[...], c[width : 2 * width]) + matmul(p[...], c[2 * width :])
     direction[...] = total[: direction.shape[0]]
@@ -115,28 +120,25 @@
     rest = running[:n_lines] - scaled[...]
     residual[...] = rest
     squares = rest * rest
-    out[0, 0] = running[n_lines:]
-    out[0, 1] = lines[...]
-    out[0, 2] = jnp.zeros((n_lines, LANES), F32)
     for b in range(n_blocks):
         at = slice(b * n_rows, (b + 1) * n_rows)
-        out[0, 2, b : b + 1] = jnp.sum(squares[at], axis=0, keepdims=True)
+        out[0, b] = running[n_lines + b * n_rows : n_lines + (b + 1) * n_rows]
+        out[0, n_blocks + b] = lines[at]
+        out[0, 2 * n_blocks, b : b + 1] = jnp.sum(squares[at], axis=0, keepdims=True)
     for z in range(1, out.shape[0]):
         out[z] = out[0]
 
 
 def gather_kernel(by_z, out, *, n_rows, n_blocks):
     n_z = by_z.shape[0]
-    n_lines = n_blocks * n_rows
     for z in range(n_z):
-        for part in range(2):
-            for b in range(n_blocks):
-                first = ((part * n_blocks + b) * n_z + z) * n_rows
-                out[0, first : first + n_rows] = by_z[z, part, b * n_rows : (b + 1) * n_rows]
-    running = by_z[0, 2]
+        for piece in range(2 * n_blocks):
+            first = (piece * n_z + z) * n_rows
+            out[0, first : first + n_rows] = by_z[z, piece]
+    running = by_z[0, 2 * n_blocks]
     for z in range(1, n_z):
-        running = running + by_z[z, 2]
-    last = 2 * n_z * n_lines
+        running = running + by_z[z, 2 * n_blocks]
+    last = 2 * n_blocks * n_z * n_rows
     out[0, last:] = jnp.zeros((out.shape[1] - last, LANES), F32)
     out[0, last : last + n_blocks] = running[:n_blocks]
     for i in range(1, out.shape[0]):
@@ -209,15 +211,23 @@
     n_lines = n_blocks * n_rows
     core = lax.axis_index("col")
     sizes = dict(n_rows=n_rows, n_blocks=n_blocks)
+    assert n_blocks == n_rows
 
     tile = hamiltonian_rows.reshape(n_z, n_x, n_rows, n_c * own_len)
     tile = tile.transpose(1, 0, 2, 3).reshape(n_x * per_block, n_c * own_len)
-    tile, correction_block = lax.optimization_barrier((tile, correction_block))
 
     own, direction = call(
         mix_kernel,
         "mix",
         (shape(own_len, 2 * width), shape(n_rows, width)),
+        call(
+            order_kernel,
+            "order",
+            shape(SUBLANES, LANES),
+            core.reshape(1),
+            in_spaces=[pltpu.SMEM],
+            cost=pl.CostEstimate(flops=10**9, transcendentals=0, bytes_accessed=0),
+        ),
         current_block,
         correction_block,
         previous_block,
@@ -253,7 +263,7 @@
     residual, mine = call(
         functools.partial(residual_kernel, **sizes),
         "residual",
-        (shape(n_lines, LANES), shape(n_z, 3, n_lines, LANES)),
+        (shape(n_lines, LANES), shape(n_z, 2 * n_blocks + 1, n_rows, LANES)),
         by_z,
         scaled,
         block_lines,

time: 128 us -> 129 us (level)
  blocking collectives: 76.5 us -> 78.4 us
    all_to_all x4, blocking collectives: 68.7 us -> 72.5 us  [exchange(): return lax.all_to_all(blocks, axis, 0, 0, tiled=True)]
    all_gather x1, blocking collectives: 7.8 us -> 5.99 us  [both_cores(): return lax.all_gather(shard, 'col')]
    pallas_call x7 -> x8, Pallas kernels: 3.09 us -> 3.14 us  [call(): pl.pallas_call(kernel, in_specs=[pl.BlockSpec(memory_space=space) for spa...]
  transfers between devices with their start and end apart: 1 -> 1, of which waited for: 1 -> 0; matrix products, arithmetic and copies ran while one was open for 0% -> 1% of each run, Pallas kernels for 0% -> 0%
where the time goes in v8:
time: 129 us
  blocking collectives  78.4 us (61%)
  starting transfers between devices  43.4 us (34%)
  Pallas kernels  3.14 us (2%)
  local copies, waits for them, and re-layouts  2.37 us (2%)
    all_to_all x4, blocking collectives, exchange(): return lax.all_to_all(blocks, axis, 0, 0, tiled=True)  72.5 us
    ppermute x1, starting transfers between devices, swap_cores(): return lax.ppermute(shard, 'col', [(0, 1), (1, 0)])  43.4 us
    all_gather x1, blocking collectives, both_cores(): return lax.all_gather(shard, 'col')  5.99 us
    pallas_call x8, Pallas kernels, call(): pl.pallas_call(kernel, in_specs=[pl.BlockSpec(memory_space=space) for spa...  3.14 us
  transfers between devices with their start and end apart: 1, of which 0 were waited for; matrix products, arithmetic and copies ran while one was open for 1% of the time, Pallas kernels for 0%

profile of v8, /device:TPU:65, one launch (start us, length us, event | category | flops | bytes accessed | tf_op | source)
XLA Modules:
  0.0 128.7 jit_solution(3988079218179411641)
XLA Ops:
  0.6 0.0 copy-start
  0.6 0.0 copy-start.1
  0.7 0.0 copy-start.2
  0.7 0.0 copy-start.3
  0.7 1.1 copy-done
  1.8 0.1 copy-done.1
  1.8 0.1 copy-done.2
  1.9 0.1 copy-done.3
  2.0 0.0 copy-start.4
  2.0 0.9 mix.1
  2.9 43.4 %collective-permute-start = (f32[256,512]{1,0:T(8,128)S(1)}, f32[256,512]{1,0:T(8,128)S(1)}, u32[]{:S(2)}, u32[]{:S(2)}) collective-permute-start(f32[256,512]{1,0:T(8,128)S(1)} %get-tuple-element.12.own), channel_id=1, source_target_pairs={{0,1},{1,0},{2,3},{3,2},{4,5},{5,4},{6,7},{7,6},{8,9},{9,8},{10,11... | collective-permute-start | bytes 1572872 | tf_op jit(solution)/shard_map/ppermute | solution.py:28
  46.3 0.0 copy-done.4
  46.3 0.4 reshape.23.tile
  46.7 0.0 copy-start.5
  46.7 0.7 copy-done.5
  47.4 0.6 fusion.part
  48.0 0.0 collective-permute-done.other
  48.0 0.6 partial.1
  48.6 20.4 %all_to_all.20.by_x = f32[8,128,128]{2,1,0:T(8,128)S(1)} all-to-all(f32[8,128,128]{2,1,0:T(8,128)S(1)} %get-tuple-element.13), channel_id=1, replica_groups=mesh['chan'=2,'row_0'=16,'row_1'=8,'col'=2] {'row_1'}, dimensions={0} | all-to-all | bytes 1048576 | tf_op jit(solution)/shard_map/all_to_all | solution.py:24
  69.0 0.1 sum_x.1
  69.1 18.9 %all_to_all.21.by_z = f32[16,8,128]{2,1,0:T(8,128)S(1)} all-to-all(f32[16,8,128]{2,1,0:T(8,128)S(1)} %sum_x.1), channel_id=1, replica_groups=mesh['chan'=2,'row_0'=16,'row_1'=8,'col'=2] {'row_0'}, dimensions={0} | all-to-all | bytes 131072 | tf_op jit(solution)/shard_map/all_to_all | solution.py:24
  88.0 15.4 %all_to_all.22.by_z = f32[16,5,2,128]{3,2,1,0:T(2,128)S(1)} all-to-all(f32[16,5,2,128]{3,2,1,0:T(2,128)S(1)} %get-tuple-element.16), channel_id=1, replica_groups=mesh['chan'=2,'row_0'=16,'row_1'=8,'col'=2] {'row_0'}, dimensions={0} | all-to-all | bytes 163840 | tf_op jit(solution)/shard_map/all_to_all | solution.py:24
  103.5 0.1 gather.1
  103.5 17.7 %all_to_all.23.lines = f32[8,136,128]{2,1,0:T(8,128)S(1)} all-to-all(f32[8,136,128]{2,1,0:T(8,128)S(1)} %gather.1), channel_id=1, replica_groups=mesh['chan'=2,'row_0'=16,'row_1'=8,'col'=2] {'row_1'}, dimensions={0} | all-to-all | bytes 1114112 | tf_op jit(solution)/shard_map/all_to_all | solution.py:24
  121.3 0.6 own_grams.1
  121.9 6.0 %all-gather = f32[1808,128]{1,0:T(8,128)S(1)} all-gather(f32[904,128]{1,0:T(8,128)S(1)} %own_grams.1), channel_id=2, replica_groups=mesh['chan'=2,'row_0'=16,'row_1'=8,'col'=2] {'col'}, dimensions={0}, use_global_device_ids=true | all-gather | bytes 1388544 | tf_op jit(solution)/shard_map/all_gather | solution.py:51
  127.9 0.8 final.1
  (4 shorter events, 0.1 us)
Async XLA Ops:
  0.6 1.1 copy-start
  0.6 1.2 copy-start.1
  0.7 1.2 copy-start.2
  0.7 1.3 %copy-start.3 = (f32[256,256]{1,0:T(8,128)S(1)}, f32[256,256]{1,0:T(8,128)}, u32[]{:S(2)}) copy-start(f32[256,256]{1,0:T(8,128)} %p.1) | copy-start | bytes 786436
  2.0 44.3 %copy-start.4 = (f32[128,1,2,512]{3,2,1,0:T(2,128)S(1)}, f32[128,1,2,512]{3,2,1,0:T(2,128)}, u32[]{:S(2)}) copy-start(f32[128,1,2,512]{3,2,1,0:T(2,128)} %param.6) | copy-start | bytes 1572868
  2.9 45.1 %collective-permute-start = (f32[256,512]{1,0:T(8,128)S(1)}, f32[256,512]{1,0:T(8,128)S(1)}, u32[]{:S(2)}, u32[]{:S(2)}) collective-permute-start(f32[256,512]{1,0:T(8,128)S(1)} %get-tuple-element.12.own), channel_id=1, source_target_pairs={{0,1},{1,0},{2,3},{3,2},{4,5},{5,4},{6,7},{7,6},{8,9},{9,8},{10,11... | collective-permute-start | bytes 1572872 | tf_op jit(solution)/shard_map/ppermute | solution.py:28
  46.7 0.7 copy-start.5

commit v9 on v7

--- a/solution.py
+++ b/solution.py
@@ -32,7 +32,7 @@
     return jnp.dot(left, right, preferred_element_type=F32, precision=lax.Precision.HIGHEST)
 
 
-def call(kernel, name, out_shape, *args, in_spaces=None, scratch=()):
+def call(kernel, name, out_shape, *args, in_spaces=None, scratch=(), cost=None):
     spaces = in_spaces or [pltpu.VMEM] * len(args)
     resident = pl.BlockSpec(memory_space=pltpu.VMEM)
     return pl.pallas_call(
@@ -42,6 +42,7 @@
         out_shape=out_shape,
         scratch_shapes=scratch,
         compiler_params=pltpu.CompilerParams(vmem_limit_bytes=VMEM_BYTES),
+        cost_estimate=cost,
         name=name,
     )(*args)
 
@@ -54,7 +55,11 @@
     return -(-count // SUBLANES) * SUBLANES
 
 
-def mix_kernel(x, w, p, c, own, direction):
+def order_kernel(core, out):
+    out[...] = jnp.full(out.shape, core[0].astype(F32))
+
+
+def mix_kernel(order, x, w, p, c, own, direction):
     width = x.shape[1]
     total = matmul(w[...], c[width : 2 * width]) + matmul(p[...], c[2 * width :])
     direction[...] = total[: direction.shape[0]]
@@ -212,12 +217,19 @@
 
     tile = hamiltonian_rows.reshape(n_z, n_x, n_rows, n_c * own_len)
     tile = tile.transpose(1, 0, 2, 3).reshape(n_x * per_block, n_c * own_len)
-    tile, correction_block = lax.optimization_barrier((tile, correction_block))
 
     own, direction = call(
         mix_kernel,
         "mix",
         (shape(own_len, 2 * width), shape(n_rows, width)),
+        call(
+            order_kernel,
+            "order",
+            shape(SUBLANES, LANES),
+            core.reshape(1),
+            in_spaces=[pltpu.SMEM],
+            cost=pl.CostEstimate(flops=10**9, transcendentals=0, bytes_accessed=0),
+        ),
         current_block,
         correction_block,
         previous_block,

time: 128 us -> 129 us (level)
  blocking collectives: 76.5 us -> 78.5 us
    all_to_all x4, blocking collectives: 68.7 us -> 72.4 us  [exchange(): return lax.all_to_all(blocks, axis, 0, 0, tiled=True)]
    all_gather x1, blocking collectives: 7.8 us -> 6.06 us  [both_cores(): return lax.all_gather(shard, 'col')]
    pallas_call x7 -> x8, Pallas kernels: 3.09 us -> 3.14 us  [call(): pl.pallas_call(kernel, in_specs=[pl.BlockSpec(memory_space=space) for spa...]
  transfers between devices with their start and end apart: 1 -> 1, of which waited for: 1 -> 0; matrix products, arithmetic and copies ran while one was open for 0% -> 1% of each run, Pallas kernels for 0% -> 0%
where the time goes in v9:
time: 129 us
  blocking collectives  78.5 us (61%)
  starting transfers between devices  43.4 us (34%)
  Pallas kernels  3.14 us (2%)
  local copies, waits for them, and re-layouts  2.37 us (2%)
    all_to_all x4, blocking collectives, exchange(): return lax.all_to_all(blocks, axis, 0, 0, tiled=True)  72.4 us
    ppermute x1, starting transfers between devices, swap_cores(): return lax.ppermute(shard, 'col', [(0, 1), (1, 0)])  43.4 us
    all_gather x1, blocking collectives, both_cores(): return lax.all_gather(shard, 'col')  6.06 us
    pallas_call x8, Pallas kernels, call(): pl.pallas_call(kernel, in_specs=[pl.BlockSpec(memory_space=space) for spa...  3.14 us
  transfers between devices with their start and end apart: 1, of which 0 were waited for; matrix products, arithmetic and copies ran while one was open for 1% of the time, Pallas kernels for 0%

profile of v9, /device:TPU:65, one launch (start us, length us, event | category | flops | bytes accessed | tf_op | source)
XLA Modules:
  0.0 128.7 jit_solution(18097317972225172952)
XLA Ops:
  0.6 0.0 copy-start
  0.6 0.0 copy-start.1
  0.7 0.0 copy-start.2
  0.7 0.0 copy-start.3
  0.7 1.1 copy-done
  1.8 0.1 copy-done.1
  1.8 0.1 copy-done.2
  1.9 0.1 copy-done.3
  2.0 0.0 copy-start.4
  2.0 0.9 mix.1
  2.9 43.4 %collective-permute-start = (f32[256,512]{1,0:T(8,128)S(1)}, f32[256,512]{1,0:T(8,128)S(1)}, u32[]{:S(2)}, u32[]{:S(2)}) collective-permute-start(f32[256,512]{1,0:T(8,128)S(1)} %get-tuple-element.12.own), channel_id=1, source_target_pairs={{0,1},{1,0},{2,3},{3,2},{4,5},{5,4},{6,7},{7,6},{8,9},{9,8},{10,11... | collective-permute-start | bytes 1572872 | tf_op jit(solution)/shard_map/ppermute | solution.py:28
  46.3 0.0 copy-done.4
  46.3 0.4 reshape.23.tile
  46.7 0.0 copy-start.5
  46.7 0.7 copy-done.5
  47.4 0.6 fusion.part
  48.0 0.0 collective-permute-done.other
  48.0 0.6 partial.1
  48.6 20.4 %all_to_all.20.by_x = f32[8,128,128]{2,1,0:T(8,128)S(1)} all-to-all(f32[8,128,128]{2,1,0:T(8,128)S(1)} %get-tuple-element.13), channel_id=1, replica_groups=mesh['chan'=2,'row_0'=16,'row_1'=8,'col'=2] {'row_1'}, dimensions={0} | all-to-all | bytes 1048576 | tf_op jit(solution)/shard_map/all_to_all | solution.py:24
  69.0 0.1 sum_x.1
  69.1 18.9 %all_to_all.21.by_z = f32[16,8,128]{2,1,0:T(8,128)S(1)} all-to-all(f32[16,8,128]{2,1,0:T(8,128)S(1)} %sum_x.1), channel_id=1, replica_groups=mesh['chan'=2,'row_0'=16,'row_1'=8,'col'=2] {'row_0'}, dimensions={0} | all-to-all | bytes 131072 | tf_op jit(solution)/shard_map/all_to_all | solution.py:24
  88.0 15.5 %all_to_all.22.by_z = f32[16,3,4,128]{3,2,1,0:T(4,128)S(1)} all-to-all(f32[16,3,4,128]{3,2,1,0:T(4,128)S(1)} %get-tuple-element.16), channel_id=1, replica_groups=mesh['chan'=2,'row_0'=16,'row_1'=8,'col'=2] {'row_0'}, dimensions={0} | all-to-all | bytes 196608 | tf_op jit(solution)/shard_map/all_to_all | solution.py:24
  103.5 0.1 gather.1
  103.5 17.7 %all_to_all.23.lines = f32[8,136,128]{2,1,0:T(8,128)S(1)} all-to-all(f32[8,136,128]{2,1,0:T(8,128)S(1)} %gather.1), channel_id=1, replica_groups=mesh['chan'=2,'row_0'=16,'row_1'=8,'col'=2] {'row_1'}, dimensions={0} | all-to-all | bytes 1114112 | tf_op jit(solution)/shard_map/all_to_all | solution.py:24
  121.2 0.6 own_grams.1
  121.8 6.1 %all-gather = f32[1808,128]{1,0:T(8,128)S(1)} all-gather(f32[904,128]{1,0:T(8,128)S(1)} %own_grams.1), channel_id=2, replica_groups=mesh['chan'=2,'row_0'=16,'row_1'=8,'col'=2] {'col'}, dimensions={0}, use_global_device_ids=true | all-gather | bytes 1388544 | tf_op jit(solution)/shard_map/all_gather | solution.py:51
  127.9 0.8 final.1
  (4 shorter events, 0.1 us)
Async XLA Ops:
  0.6 1.1 copy-start
  0.6 1.2 copy-start.1
  0.7 1.2 copy-start.2
  0.7 1.3 %copy-start.3 = (f32[256,256]{1,0:T(8,128)S(1)}, f32[256,256]{1,0:T(8,128)}, u32[]{:S(2)}) copy-start(f32[256,256]{1,0:T(8,128)} %p.1) | copy-start | bytes 786436
  2.0 44.3 %copy-start.4 = (f32[128,1,2,512]{3,2,1,0:T(2,128)S(1)}, f32[128,1,2,512]{3,2,1,0:T(2,128)}, u32[]{:S(2)}) copy-start(f32[128,1,2,512]{3,2,1,0:T(2,128)} %param.6) | copy-start | bytes 1572868
  2.9 45.1 %collective-permute-start = (f32[256,512]{1,0:T(8,128)S(1)}, f32[256,512]{1,0:T(8,128)S(1)}, u32[]{:S(2)}, u32[]{:S(2)}) collective-permute-start(f32[256,512]{1,0:T(8,128)S(1)} %get-tuple-element.12.own), channel_id=1, source_target_pairs={{0,1},{1,0},{2,3},{3,2},{4,5},{5,4},{6,7},{7,6},{8,9},{9,8},{10,11... | collective-permute-start | bytes 1572872 | tf_op jit(solution)/shard_map/ppermute | solution.py:28
  46.7 0.7 copy-start.5

commit v10 on v8

--- a/solution.py
+++ b/solution.py
@@ -32,7 +32,7 @@
     return jnp.dot(left, right, preferred_element_type=F32, precision=lax.Precision.HIGHEST)
 
 
-def call(kernel, name, out_shape, *args, in_spaces=None, scratch=(), cost=None):
+def call(kernel, name, out_shape, *args, in_spaces=None, scratch=()):
     spaces = in_spaces or [pltpu.VMEM] * len(args)
     resident = pl.BlockSpec(memory_space=pltpu.VMEM)
     return pl.pallas_call(
@@ -42,7 +42,6 @@
         out_shape=out_shape,
         scratch_shapes=scratch,
         compiler_params=pltpu.CompilerParams(vmem_limit_bytes=VMEM_BYTES),
-        cost_estimate=cost,
         name=name,
     )(*args)
 
@@ -55,11 +54,7 @@
     return -(-count // SUBLANES) * SUBLANES
 
 
-def order_kernel(core, out):
-    out[...] = jnp.full(out.shape, core[0].astype(F32))
-
-
-def mix_kernel(order, x, w, p, c, own, direction):
+def mix_kernel(x, w, p, c, own, direction):
     width = x.shape[1]
     total = matmul(w[...], c[width : 2 * width]) + matmul(p[...], c[2 * width :])
     direction[...] = total[: direction.shape[0]]
@@ -215,19 +210,12 @@
 
     tile = hamiltonian_rows.reshape(n_z, n_x, n_rows, n_c * own_len)
     tile = tile.transpose(1, 0, 2, 3).reshape(n_x * per_block, n_c * own_len)
+    tile, correction_block = lax.optimization_barrier((tile, correction_block))
 
     own, direction = call(
         mix_kernel,
         "mix",
         (shape(own_len, 2 * width), shape(n_rows, width)),
-        call(
-            order_kernel,
-            "order",
-            shape(SUBLANES, LANES),
-            core.reshape(1),
-            in_spaces=[pltpu.SMEM],
-            cost=pl.CostEstimate(flops=10**9, transcendentals=0, bytes_accessed=0),
-        ),
         current_block,
         correction_block,
         previous_block,

time: 129 us -> 128 us (level)
  blocking collectives: 78.4 us -> 76.4 us
    all_to_all x4, blocking collectives: 72.5 us -> 68.6 us  [exchange(): return lax.all_to_all(blocks, axis, 0, 0, tiled=True)]
    all_gather x1, blocking collectives: 5.99 us -> 7.8 us  [both_cores(): return lax.all_gather(shard, 'col')]
    pallas_call x8 -> x7, Pallas kernels: 3.14 us -> 3.09 us  [call(): pl.pallas_call(kernel, in_specs=[pl.BlockSpec(memory_space=space) for spa...]
  transfers between devices with their start and end apart: 1 -> 1, of which waited for: 0 -> 1; matrix products, arithmetic and copies ran while one was open for 1% -> 0% of each run, Pallas kernels for 0% -> 0%
where the time goes in v10:
time: 128 us; the launch traced here: 127 us
  blocking collectives  76.4 us (60%)
  starting transfers between devices  43.4 us (34%)
  Pallas kernels  3.09 us (2%)
  local copies, waits for them, and re-layouts  2.92 us (2%)
    all_to_all x4, blocking collectives, exchange(): return lax.all_to_all(blocks, axis, 0, 0, tiled=True)  68.6 us
    ppermute x1, starting transfers between devices, swap_cores(): return lax.ppermute(shard, 'col', [(0, 1), (1, 0)])  43.4 us
    all_gather x1, blocking collectives, both_cores(): return lax.all_gather(shard, 'col')  7.8 us
    pallas_call x7, Pallas kernels, call(): pl.pallas_call(kernel, in_specs=[pl.BlockSpec(memory_space=space) for spa...  3.09 us
  transfers between devices with their start and end apart: 1, of which 1 were waited for; matrix products, arithmetic and copies ran while one was open for 0% of the time, Pallas kernels for 0%

profile of v10, /device:TPU:65, one launch (start us, length us, event | category | flops | bytes accessed | tf_op | source)
XLA Modules:
  0.0 127.4 jit_solution(16457210251522269470)
XLA Ops:
  0.6 0.0 copy-start
  0.6 1.1 copy_bitcast_fusion
  1.8 0.0 copy-start.1
  1.8 0.0 copy-start.2
  1.8 0.0 copy-start.3
  1.8 0.4 reshape.22.tile
  2.2 0.0 copy-done
  2.2 0.6 copy-done.1
  2.8 0.1 copy-done.2
  2.9 0.1 copy-done.3
  2.9 0.9 mix.1
  3.8 43.4 %collective-permute-start = (f32[256,512]{1,0:T(8,128)S(1)}, f32[256,512]{1,0:T(8,128)S(1)}, u32[]{:S(2)}, u32[]{:S(2)}) collective-permute-start(f32[256,512]{1,0:T(8,128)S(1)} %get-tuple-element.16.own), channel_id=1, source_target_pairs={{0,1},{1,0},{2,3},{3,2},{4,5},{5,4},{6,7},{7,6},{8,9},{9,8},{10,11... | collective-permute-start | bytes 1572872 | tf_op jit(solution)/shard_map/ppermute | solution.py:28
  47.2 0.0 copy-start.4
  47.2 0.7 copy-done.4
  47.9 0.6 fusion.part
  48.5 0.2 collective-permute-done.other
  48.7 0.6 partial.1
  49.3 20.4 %all_to_all.20.by_x = f32[8,128,128]{2,1,0:T(8,128)S(1)} all-to-all(f32[8,128,128]{2,1,0:T(8,128)S(1)} %get-tuple-element.17), channel_id=1, replica_groups=mesh['chan'=2,'row_0'=16,'row_1'=8,'col'=2] {'row_1'}, dimensions={0} | all-to-all | bytes 1048576 | tf_op jit(solution)/shard_map/all_to_all | solution.py:24
  69.7 0.1 sum_x.1
  69.8 17.7 %all_to_all.21.by_z = f32[16,8,128]{2,1,0:T(8,128)S(1)} all-to-all(f32[16,8,128]{2,1,0:T(8,128)S(1)} %sum_x.1), channel_id=1, replica_groups=mesh['chan'=2,'row_0'=16,'row_1'=8,'col'=2] {'row_0'}, dimensions={0} | all-to-all | bytes 131072 | tf_op jit(solution)/shard_map/all_to_all | solution.py:24
  87.5 14.6 %all_to_all.22.by_z = f32[16,5,2,128]{3,2,1,0:T(2,128)S(1)} all-to-all(f32[16,5,2,128]{3,2,1,0:T(2,128)S(1)} %get-tuple-element.20), channel_id=1, replica_groups=mesh['chan'=2,'row_0'=16,'row_1'=8,'col'=2] {'row_0'}, dimensions={0} | all-to-all | bytes 163840 | tf_op jit(solution)/shard_map/all_to_all | solution.py:24
  102.1 0.1 gather.1
  102.2 15.9 %all_to_all.23.lines = f32[8,136,128]{2,1,0:T(8,128)S(1)} all-to-all(f32[8,136,128]{2,1,0:T(8,128)S(1)} %gather.1), channel_id=1, replica_groups=mesh['chan'=2,'row_0'=16,'row_1'=8,'col'=2] {'row_1'}, dimensions={0} | all-to-all | bytes 1114112 | tf_op jit(solution)/shard_map/all_to_all | solution.py:24
  118.1 0.6 own_grams.1
  118.7 7.8 %all-gather = f32[1808,128]{1,0:T(8,128)S(1)} all-gather(f32[904,128]{1,0:T(8,128)S(1)} %own_grams.1), channel_id=2, replica_groups=mesh['chan'=2,'row_0'=16,'row_1'=8,'col'=2] {'col'}, dimensions={0}, use_global_device_ids=true | all-gather | bytes 1388544 | tf_op jit(solution)/shard_map/all_gather | solution.py:50
  126.5 0.8 final.1
  (2 shorter events, 0.0 us)
Async XLA Ops:
  0.6 1.6 %copy-start = (f32[768,256]{1,0:T(8,128)S(1)}, f32[768,256]{1,0:T(8,128)}, u32[]{:S(2)}) copy-start(f32[768,256]{1,0:T(8,128)} %c.1) | copy-start | bytes 2359300
  1.8 1.0 copy-start.1
  1.8 1.0 copy-start.2
  1.8 1.1 copy-start.3
  3.8 44.9 %collective-permute-start = (f32[256,512]{1,0:T(8,128)S(1)}, f32[256,512]{1,0:T(8,128)S(1)}, u32[]{:S(2)}, u32[]{:S(2)}) collective-permute-start(f32[256,512]{1,0:T(8,128)S(1)} %get-tuple-element.16.own), channel_id=1, source_target_pairs={{0,1},{1,0},{2,3},{3,2},{4,5},{5,4},{6,7},{7,6},{8,9},{9,8},{10,11... | collective-permute-start | bytes 1572872 | tf_op jit(solution)/shard_map/ppermute | solution.py:28
  47.2 0.7 copy-start.4
